TPU v7x, 32 devices: a whole 2x2x4 slice. The times are simulated.
32 devices in a mesh: node: 4 (over z), local: 8 (over y, x, core).
Axes of the slice: x: 2, y: 2, z: 4, core: 2. Of those that a mesh axis runs over, the one named last changes fastest.
Arguments:
- tokens: bfloat16 [512, 7168], P(('node', 'local')), may hold values from -6 to 6
- grad_out: bfloat16 [512, 7168], P(('node', 'local')), may hold values from -6 to 6
- gates: bfloat16 [512, 3], P(('node', 'local')), may hold values from 0.19921875 to 1
- expert_ids: int32 [512, 3], P(('node', 'local')), may hold values from 0 to 7, as said below
- w_gate: bfloat16 [4, 7168, 2048], P('node', None, 'local'), may hold values from -0.0625 to 0.0625
- w_up: bfloat16 [4, 7168, 2048], P('node', None, 'local'), may hold values from -0.0625 to 0.0625
- w_down: bfloat16 [4, 7168, 2048], P('node', None, 'local'), may hold values from -0.1875 to 0.1875
- s_gate: bfloat16 [7168, 2048], P(None, 'local'), may hold values from -0.0625 to 0.0625
- s_up: bfloat16 [7168, 2048], P(None, 'local'), may hold values from -0.0625 to 0.0625
- s_down: bfloat16 [7168, 2048], P(None, 'local'), may hold values from -0.125 to 0.125
Outputs:
- dx: bfloat16 [512, 7168], P(('node', 'local'))
- dgates: float32 [512, 3], P(('node', 'local'))
- d_w_gate: bfloat16 [4, 7168, 2048], P('node', None, 'local')
- d_w_up: bfloat16 [4, 7168, 2048], P('node', None, 'local')
- d_w_down: bfloat16 [4, 7168, 2048], P('node', None, 'local')
- d_s_gate: bfloat16 [7168, 2048], P('node', 'local')
- d_s_up: bfloat16 [7168, 2048], P('node', 'local')
- d_s_down: bfloat16 [7168, 2048], P('node', 'local')
Inputs may be any that keep to these rules, and one draw needn't show every extreme that they name: `expert_ids`: each token names both experts of one node and one expert of a second node. Of the tokens of one device exactly 8 name experts of each node and at most 8 name any one expert; for every node one of its experts is named by exactly 8 tokens of every device.
All inputs are finite; a program needn't handle non-finite values.
Results may differ from a plain program's by a relative error of at most 0.014.
Values may be sent and summed in bfloat16 or wider, within the bound.
A program may use at most 192 MiB of HBM per device.

v0:
```python
import functools

import jax
import jax.numpy as jnp
from jax import lax
from jax.experimental import pallas as pl
from jax.experimental.pallas import tpu as pltpu
from jax.sharding import PartitionSpec as P

E_NODE = 2
LANES = 128
MESH = pl.DeviceIdType.MESH


def bit_orders(local_count):
    bits = local_count.bit_length() - 1
    outer = list(range(1, bits))
    forward = [1 << b for b in outer] + [1]
    backward = [1 << b for b in outer[::-1]] + [1]
    return (forward, backward)


def near_first(node_count):
    return sorted(range(1, node_count), key=lambda s: min(s, node_count - s))


def greet(node_count, masks):
    n, l = lax.axis_index("node"), lax.axis_index("local")
    barrier = pltpu.get_barrier_semaphore()
    for r in range(1, node_count):
        pl.semaphore_signal(
            barrier, inc=1, device_id=(lax.rem(n + r, node_count), l), device_id_type=MESH
        )
    for mask in masks:
        pl.semaphore_signal(barrier, inc=1, device_id=(n, l ^ mask), device_id_type=MESH)
    pl.semaphore_wait(barrier, node_count - 1 + len(masks))


def gather_kernel(
    node_count, orders, tok, grad, sel_t, sel_g, meta,
    all_t, all_g, ext_t, ext_g, all_m, send_sem, recv_sem, own_sem,
):
    n, l = lax.axis_index("node"), lax.axis_index("local")
    forward, backward = orders
    stages = len(forward)
    own_blocks = tok.shape[0]
    part = ext_t.shape[-1]
    greet(node_count, forward)
    counter = [0]
    sends = []

    def remote(src, dst, device):
        i = counter[0]
        counter[0] += 1
        copy = pltpu.make_async_remote_copy(
            src_ref=src, dst_ref=dst, send_sem=send_sem.at[i], recv_sem=recv_sem.at[i],
            device_id=device, device_id_type=MESH,
        )
        copy.start()
        sends.append(copy)
        return copy

    fills = [
        pltpu.make_async_copy(tok, all_t.at[0, pl.ds(0, own_blocks)], own_sem.at[0]),
        pltpu.make_async_copy(grad, all_g.at[0, pl.ds(0, own_blocks)], own_sem.at[1]),
        pltpu.make_async_copy(meta.at[0], all_m.at[0, 0], own_sem.at[2]),
    ]
    for fill in fills:
        fill.start()

    def view(buf, s, start, size):
        if buf is all_t or buf is all_g:
            if s == 0:
                return buf.at[pl.ds(start, size), pl.ds(0, own_blocks)]
            return buf.at[pl.ds(start, size), own_blocks + s - 1]
        if buf is all_m:
            return buf.at[s, pl.ds(start, size)]
        return buf.at[s - 1, pl.ds(start, size)]

    arrived = {}
    order = near_first(node_count)
    for s in order:
        r = node_count - s
        m = lax.rem(n + r, node_count)
        columns = pl.ds(pl.multiple_of(m * part, LANES), part)
        arrived[s] = [
            remote(meta.at[r], all_m.at[s, 0], (m, l)),
            remote(sel_t.at[r - 1], all_t.at[0, own_blocks + s - 1], (m, l)),
            remote(sel_g.at[r - 1], all_g.at[0, own_blocks + s - 1], (m, l)),
            remote(tok.at[:, :, columns], ext_t.at[s - 1, 0], (m, l)),
            remote(grad.at[:, :, columns], ext_g.at[s - 1, 0], (m, l)),
        ]
    for fill in fills:
        fill.wait()

    items = [0] + order
    pending = {}

    def issue(item, stage):
        s = items[item]
        bufs = [(all_m, forward), (all_t, forward), (all_g, backward)]
        if s > 0:
            bufs += [(ext_t, forward), (ext_g, backward)]
        if stage > 0:
            before = pending[item]
        else:
            before = arrived.get(s, [])
        for copy in before:
            copy.wait_recv()
        size = 1 << stage
        pending[item] = [
            remote(view(buf, s, 0, size), view(buf, s, size, size), (n, l ^ bits[stage]))
            for buf, bits in bufs
        ]

    for tick in range(len(items) + stages - 1):
        for item in range(len(items)):
            stage = tick - item
            if 0 <= stage < stages:
                issue(item, stage)
    for item in range(len(items)):
        for copy in pending[item]:
            copy.wait_recv()
    for copy in sends:
        copy.wait_send()


def gather_rows(node_count, local_count, tok, grad, sel_t, sel_g, meta):
    own_blocks, cap, width = tok.shape
    orders = bit_orders(local_count)
    part = width // node_count
    copies = len(orders[0]) * (3 + 5 * (node_count - 1)) + 5 * (node_count - 1)
    rows = (local_count, own_blocks + node_count - 1, cap, width)
    ext = (node_count - 1, local_count, own_blocks, cap, part)
    bf16 = jnp.bfloat16
    vmem = pl.BlockSpec(memory_space=pltpu.VMEM)
    hbm = pl.BlockSpec(memory_space=pl.ANY)
    return pl.pallas_call(
        functools.partial(gather_kernel, node_count, orders),
        out_shape=[
            jax.ShapeDtypeStruct(rows, bf16),
            jax.ShapeDtypeStruct(rows, bf16),
            jax.ShapeDtypeStruct(ext, bf16),
            jax.ShapeDtypeStruct(ext, bf16),
            jax.ShapeDtypeStruct((node_count, local_count) + meta.shape[1:], bf16),
        ],
        in_specs=[vmem] * 5,
        out_specs=[hbm] * 5,
        scratch_shapes=[
            pltpu.SemaphoreType.DMA((copies,)),
            pltpu.SemaphoreType.DMA((copies,)),
            pltpu.SemaphoreType.DMA((3,)),
        ],
        compiler_params=pltpu.CompilerParams(collective_id=0, has_side_effects=True),
        name="gather_rows",
    )(tok, grad, sel_t, sel_g, meta)


def reduce_kernel(node_count, forward, own_blocks, part_ref, rows_t, rows_g, gg, gu, gh, pack,
                  own_ref, home_ref, packs, dw_g, dw_u, dw_d,
                  acc, land, back, held_t, held_g, grads,
                  send_sem, recv_sem, zsend_sem, zrecv_sem, psend_sem, precv_sem, load_sem, out_sem):
    n, l = lax.axis_index("node"), lax.axis_index("local")
    count, blocks, cap, width = part_ref.shape
    stages = len(forward)
    half = width // 2 // LANES * LANES
    load = pltpu.make_async_copy(part_ref, acc, load_sem.at[0])
    load.start()
    load_t = pltpu.make_async_copy(rows_t, held_t, load_sem.at[1])
    load_t.start()
    load_g = pltpu.make_async_copy(rows_g, held_g, load_sem.at[2])
    load_g.start()
    greet(node_count, forward)
    passed = []
    for s in near_first(node_count):
        copy = pltpu.make_async_remote_copy(
            src_ref=pack, dst_ref=packs.at[node_count - s - 1],
            send_sem=psend_sem.at[s - 1], recv_sem=precv_sem.at[node_count - s - 1],
            device_id=(lax.rem(n + s, node_count), l), device_id_type=MESH,
        )
        copy.start()
        passed.append(copy)
    load.wait()
    tile = 4 * LANES
    work = [(load_t, held_t, gg, dw_g), (None, held_t, gu, dw_u), (load_g, held_g, gh, dw_d)]
    stored = []

    def multiply(index):
        ready, held, right, out = work[index]
        if ready is not None:
            ready.wait()

        def step(c, carry):
            at = pl.ds(pl.multiple_of(c * tile, tile), tile)
            grads[index, at, :] = contract_first(held[:, at], right[...]).astype(jnp.bfloat16)
            return carry

        lax.fori_loop(0, held.shape[1] // tile, step, 0)
        copy = pltpu.make_async_copy(grads.at[index], out, out_sem.at[index])
        copy.start()
        stored.append(copy)

    groups = [(own_blocks, blocks - own_blocks), (0, own_blocks)]
    bands = [(0, half), (half, width - half)]
    top = stages - 1
    plans = [[top] + list(range(top))[::-1], [top] + list(range(top))]
    counter = [0]
    sends = []
    keep = {key: list(range(count)) for key in [(g, b) for g in range(2) for b in range(2)]}
    flight = {}

    def start(g, b, stage):
        bit = 1 << plans[b][stage]
        first, size = groups[g]
        columns = pl.ds(*bands[b])
        out = [p for p in keep[g, b] if p & bit]
        stay = [p for p in keep[g, b] if not p & bit]
        keep[g, b] = stay
        copies = []
        for p in out:
            i = counter[0]
            counter[0] += 1
            copy = pltpu.make_async_remote_copy(
                src_ref=acc.at[p, pl.ds(first, size), :, columns],
                dst_ref=land.at[p, pl.ds(first, size), :, columns],
                send_sem=send_sem.at[i], recv_sem=recv_sem.at[i],
                device_id=(n, l ^ forward[plans[b][stage]]), device_id_type=MESH,
            )
            copy.start()
            sends.append(copy)
            copies.append((p, copy))
        flight[g, b] = (bit, copies)

    def settle(g, b):
        first, size = groups[g]
        columns = pl.ds(*bands[b])
        bit, copies = flight[g, b]
        for p, copy in copies:
            copy.wait_recv()
            q = p ^ bit

            def add(k, carry, p=p, q=q):
                there = land[p, first + k, :, columns].astype(jnp.float32)
                here = acc[q, first + k, :, columns].astype(jnp.float32)
                acc[q, first + k, :, columns] = (here + there).astype(jnp.bfloat16)
                return carry

            lax.fori_loop(0, size, add, 0)

    homes = []
    for stage in range(stages + 1):
        for g in range(2):
            for b in range(2):
                if stage > 0:
                    settle(g, b)
                if stage < stages:
                    start(g, b, stage)
            if stage == stages and g == 0:
                for s in near_first(node_count):
                    copy = pltpu.make_async_remote_copy(
                        src_ref=acc.at[0, own_blocks + s - 1],
                        dst_ref=back.at[node_count - s - 1],
                        send_sem=zsend_sem.at[s - 1],
                        recv_sem=zrecv_sem.at[node_count - s - 1],
                        device_id=(lax.rem(n + s, node_count), l), device_id_type=MESH,
                    )
                    copy.start()
                    homes.append(copy)
        if stage < len(work):
            multiply(stage)
    for index in range(stages + 1, len(work)):
        multiply(index)
    own_ref[...] = acc[0, pl.ds(0, own_blocks)]
    for copy in homes:
        copy.wait_recv()
    home_ref[...] = back[...]
    for copy in passed:
        copy.wait_recv()
    for copy in sends + homes + passed:
        copy.wait_send()
    for copy in stored:
        copy.wait()


def reduce_rows(node_count, local_count, part, rows_t, rows_g, gg, gu, gh, pack):
    count, blocks, cap, width = part.shape
    forward = bit_orders(local_count)[0]
    own_blocks = blocks - (node_count - 1)
    bf16 = jnp.bfloat16
    vmem = pl.BlockSpec(memory_space=pltpu.VMEM)
    hbm = pl.BlockSpec(memory_space=pl.ANY)
    copies = 4 * (local_count - 1)
    grad = (rows_t.shape[1], gg.shape[1])
    return pl.pallas_call(
        functools.partial(reduce_kernel, node_count, forward, own_blocks),
        out_shape=[
            jax.ShapeDtypeStruct((own_blocks, cap, width), bf16),
            jax.ShapeDtypeStruct((node_count - 1, cap, width), bf16),
            jax.ShapeDtypeStruct((node_count - 1,) + pack.shape, bf16),
        ] + [jax.ShapeDtypeStruct(grad, bf16)] * 3,
        in_specs=[hbm] * 3 + [vmem] * 4,
        out_specs=[vmem] * 2 + [hbm] * 4,
        scratch_shapes=[
            pltpu.VMEM(part.shape, bf16),
            pltpu.VMEM(part.shape, bf16),
            pltpu.VMEM((node_count - 1, cap, width), bf16),
            pltpu.VMEM(rows_t.shape, bf16),
            pltpu.VMEM(rows_g.shape, bf16),
            pltpu.VMEM((3,) + grad, bf16),
            pltpu.SemaphoreType.DMA((copies,)),
            pltpu.SemaphoreType.DMA((copies,)),
            pltpu.SemaphoreType.DMA((node_count - 1,)),
            pltpu.SemaphoreType.DMA((node_count - 1,)),
            pltpu.SemaphoreType.DMA((node_count - 1,)),
            pltpu.SemaphoreType.DMA((node_count - 1,)),
            pltpu.SemaphoreType.DMA((3,)),
            pltpu.SemaphoreType.DMA((3,)),
        ],
        compiler_params=pltpu.CompilerParams(collective_id=1, has_side_effects=True),
        name="reduce_rows",
    )(part, rows_t, rows_g, gg, gu, gh, pack)


def silu_parts(pre_gate):
    sig = jax.nn.sigmoid(pre_gate)
    return (pre_gate * sig, sig * (1.0 + pre_gate * (1.0 - sig)))


def dot(left, right):
    return jnp.dot(left, right, preferred_element_type=jnp.float32)


def contract_first(left, right):
    return lax.dot_general(
        left, right, (((0,), (0,)), ((), ())), preferred_element_type=jnp.float32
    )


def contract_last(left, right):
    return lax.dot_general(
        left, right, (((1,), (1,)), ((), ())), preferred_element_type=jnp.float32
    )


def flip(values, local_count):
    bits = local_count.bit_length() - 1
    shaped = values.reshape((2,) * bits + (-1,) + values.shape[1:])
    axes = (0,) + tuple(range(1, bits))[::-1] + tuple(range(bits, shaped.ndim))
    return jnp.transpose(shaped, axes).reshape(values.shape)


def ffn_backward(pre_gate, pre_up, upstream, weight):
    activ, slope = silu_parts(pre_gate)
    hidden = activ * pre_up
    scaled = weight * upstream
    grad_up = (scaled * activ).astype(jnp.bfloat16)
    grad_gate = (scaled * pre_up * slope).astype(jnp.bfloat16)
    weighted = (weight * hidden).astype(jnp.bfloat16)
    return (grad_gate, grad_up, weighted, hidden * upstream)


def local(tokens, grad_out, gates, expert_ids, w_gate, w_up, w_down, s_gate, s_up, s_down):
    held, width = tokens.shape
    nodes, locals_ = lax.axis_size("node"), lax.axis_size("local")
    n, l = lax.axis_index("node"), lax.axis_index("local")
    cap = 2 * held // nodes
    own_blocks = held // cap
    bf16, f32 = jnp.bfloat16, jnp.float32

    rel = lax.rem(expert_ids // E_NODE - n + nodes, nodes)
    near = jnp.arange(nodes, dtype=jnp.int32)
    hit_k = rel[:, :, None] == near
    hit = jnp.any(hit_k, axis=1)
    lower = jnp.tril(jnp.ones((held, held), f32))
    rank = dot(lower, hit.astype(f32)).astype(jnp.int32) - 1
    slots = jnp.arange(cap, dtype=jnp.int32)
    pick = hit[:, :, None] & (rank[:, :, None] == slots)
    which = (lax.rem(expert_ids, E_NODE)[:, :, None] == jnp.arange(E_NODE)) & True
    named = hit_k[:, :, :, None] & which[:, :, None, :]
    weight = jnp.sum(jnp.where(named, gates.astype(f32)[:, :, None, None], 0.0), axis=1)
    rows = pick[:, 1:].astype(bf16)
    sel_t = jnp.einsum("trc,td->rcd", rows, tokens, preferred_element_type=f32).astype(bf16)
    sel_g = jnp.einsum("trc,td->rcd", rows, grad_out, preferred_element_type=f32).astype(bf16)
    slot_w = jnp.sum(jnp.where(pick[:, 1:, :, None], weight[:, 1:, None, :], 0.0), axis=0)
    meta = jnp.zeros((nodes, held, LANES), f32)
    meta = meta.at[0, :, :E_NODE].set(weight[:, 0])
    meta = meta.at[1:, :cap, :E_NODE].set(slot_w).astype(bf16)

    all_t, all_g, ext_t, ext_g, all_m = gather_rows(
        nodes, locals_,
        tokens.reshape(own_blocks, cap, width), grad_out.reshape(own_blocks, cap, width),
        sel_t, sel_g, meta,
    )
    total = locals_ * (held + (nodes - 1) * cap)
    rows_t, rows_g = all_t.reshape(total, width), all_g.reshape(total, width)
    units = s_gate.shape[1]

    def own(values):
        return values.reshape(locals_, -1, values.shape[-1])[:, :held].reshape(
            locals_ * held, values.shape[-1]
        )

    pre_gate, pre_up = dot(rows_t, s_gate), dot(rows_t, s_up)
    upstream = flip(dot(rows_g, s_down), locals_)
    sg, su, sh, _ = ffn_backward(own(pre_gate), own(pre_up), own(upstream), 1.0)
    pack = jnp.concatenate([sg, su, flip(sh, locals_)], axis=1)
    expert = l // (locals_ // E_NODE)
    table = jnp.concatenate([all_m[0, :, :, :E_NODE]] + [
        all_m[s, :, :cap, :E_NODE] for s in range(1, nodes)
    ], axis=1).reshape(total, E_NODE).astype(f32)
    mine = jnp.arange(E_NODE) == expert
    row_w = jnp.sum(jnp.where(mine, table, 0.0), axis=1, keepdims=True)
    gate_w, up_w, down_w = w_gate[0], w_up[0], w_down[0]
    gg, gu, gh, product = ffn_backward(
        dot(rows_t, gate_w), dot(rows_t, up_w), flip(dot(rows_g, down_w), locals_), row_w
    )

    def widen(values):
        return jnp.pad(
            values.reshape(locals_, held, -1), ((0, 0), (0, (nodes - 1) * cap), (0, 0))
        ).reshape(total, -1)

    partial_dx = (
        contract_last(gg, gate_w) + contract_last(gu, up_w)
        + contract_last(widen(sg), s_gate) + contract_last(widen(su), s_up)
    ).astype(bf16)
    score = jnp.sum(product, axis=1, keepdims=True)
    lane = jnp.arange(LANES)
    score = jnp.where(lane == expert, score, 0.0).astype(bf16)
    part = jnp.concatenate([partial_dx, score], axis=1).reshape(
        locals_, own_blocks + nodes - 1, cap, width + LANES
    )
    own_sum, home, packs, *dw = reduce_rows(
        nodes, locals_, part, rows_t, rows_g, gg, gu, flip(gh, locals_), pack
    )
    expert_grads = tuple(g[None] for g in dw)
    piece = width // nodes
    start = n * piece
    here_t = own(lax.dynamic_slice_in_dim(rows_t, start, piece, 1))
    here_g = own(lax.dynamic_slice_in_dim(rows_g, start, piece, 1))
    every_t = jnp.concatenate([here_t, ext_t.reshape(-1, piece)], axis=0)
    every_g = jnp.concatenate([here_g, ext_g.reshape(-1, piece)], axis=0)
    packed = jnp.concatenate([pack, packs.reshape(-1, pack.shape[1])], axis=0)
    shared_grads = (
        contract_first(every_t, packed[:, :units]).astype(bf16),
        contract_first(every_t, packed[:, units : 2 * units]).astype(bf16),
        contract_first(every_g, packed[:, 2 * units :]).astype(bf16),
    )

    own_rows = own_sum.reshape(held, width + LANES).astype(f32)
    home_rows = jnp.einsum("trc,rcd->td", rows, home[:, :, :width], preferred_element_type=f32)
    dx = (own_rows[:, :width] + home_rows).astype(bf16)
    home_score = jnp.sum(
        jnp.where(pick[:, 1:, :, None], home[None, :, :, width : width + E_NODE].astype(f32), 0.0),
        axis=2,
    )
    scores = jnp.concatenate([own_rows[:, None, width : width + E_NODE], home_score], axis=1)
    dgates = jnp.sum(jnp.where(named, scores[:, None], 0.0), axis=(2, 3))
    return (dx, dgates) + expert_grads + shared_grads


def solution(mesh):
    token = P(("node", "local"), None)
    routed = P("node", None, "local")
    shared = P(None, "local")
    shared_out = P("node", "local")
    return jax.shard_map(
        local,
        mesh=mesh,
        in_specs=(token,) * 4 + (routed,) * 3 + (shared,) * 3,
        out_specs=(token,) * 2 + (routed,) * 3 + (shared_out,) * 3,
        check_vma=False,
    )
```

profile of v0, /device:TPU:0, one launch (start us, length us, event | category | flops | bytes accessed | tf_op | source)
XLA Modules:
  0.0 173.8 jit_solution(12360530901470655045)
XLA Ops:
  0.6 0.7 negate_select_fusion.3
  1.5 0.7 convert_element_type.80
  2.9 1.9 %convolution_convert_fusion.sel_g = bf16[3,8,7168]{2,1,0:T(8,128)(2,1)} fusion(bf16[16,7168]{1,0:T(8,128)(2,1)} %param.15, s32[16,4]{0,1:T(4,128)S(1)} %fusion.29, pred[16,4]{0,1:T(4,128)(4,1)S(1)} %get-tuple-element.54), kind=kOutput, calls=%fused_computation.4 | convolution fusion | flops 5678080 | bytes 573760 | tf_op jit(solution)/shard_map/trc,td->rcd/dot_general | solution.py:383
  4.8 1.9 %convolution_convert_fusion.1.sel_t = bf16[3,8,7168]{2,1,0:T(8,128)(2,1)} fusion(bf16[16,7168]{1,0:T(8,128)(2,1)} %param.14, s32[16,4]{0,1:T(4,128)S(1)} %fusion.29, pred[16,4]{0,1:T(4,128)(4,1)S(1)} %get-tuple-element.54), kind=kOutput, calls=%fused_computation.5 | convolution fusion | flops 5678080 | bytes 573760 | tf_op jit(solution)/shard_map/trc,td->rcd/dot_general | solution.py:382
  6.7 64.9 %gather_rows.1 = (bf16[8,5,8,7168]{3,2,1,0:T(8,128)(2,1)}, bf16[8,5,8,7168]{3,2,1,0:T(8,128)(2,1)}, bf16[3,8,2,8,1792]{4,3,2,1,0:T(8,128)(2,1)}, bf16[3,8,2,8,17...) custom-call(bf16[2,8,7168]{2,1,0:T(8,128)(2,1)} %bitcast.158, bf16[2,8,7168]{2,1,0:T(8,128)(2,1)} %bitcast.159, ...), custom_call_target="tpu_custom_call" | custom-call | tf_op jit(solution)/shard_map/gather_rows/pallas_call | solution.py:138
  71.6 3.4 %fusion.7 = f32[8,16,256]{2,1,0:T(8,128)S(1)} fusion(bf16[7168,256]{1,0:T(8,128)(2,1)} %param.21, bf16[8,40,7168]{2,1,0:T(8,128)(2,1)} %bitcast.137), kind=kOutput, calls=%fused_computation.14 | convolution fusion | flops 469762048 | bytes 5636096 | tf_op jit(solution)/shard_map/dot_general | solution.py:330
  75.5 2.9 %fusion.9 = f32[8,16,256]{2,1,0:T(8,128)S(1)} fusion(bf16[7168,256]{1,0:T(8,128)(2,1)} %param.22, bf16[8,40,7168]{2,1,0:T(8,128)(2,1)S(1)} %bitcast.141), kind=kOutput, calls=%fused_computation.16 | convolution fusion | flops 469762048 | bytes 5636096 | tf_op jit(solution)/shard_map/dot_general | solution.py:330
  78.4 0.8 copy-done.1
  79.2 1.5 fusion.26
  80.8 0.7 multiply_convert_fusion.3
  81.7 0.7 pad_maximum_fusion.5.pack
  83.1 4.9 %fusion.13 = f32[320,256]{1,0:T(8,128)S(1)} fusion(bf16[320,7168]{1,0:T(8,128)(2,1)} %bitcast.138, bf16[1,7168,256]{2,1,0:T(8,128)(2,1)} %param.18), kind=kOutput, calls=%fused_computation.20 | convolution fusion | flops 1174405120 | bytes 8585216 | tf_op jit(solution)/shard_map/dot_general | solution.py:330
  88.1 3.8 %fusion.23 = f32[2,2,2,40,256]{4,3,1,2,0:T(8,128)S(1)} fusion(bf16[2,2,2,40,7168]{4,3,2,1,0:T(8,128)(2,1)} %bitcast.145, bf16[1,7168,256]{2,1,0:T(8,128)(2,1)S(1)} %copy-done.21), kind=kOutput, calls=%fused_computation.34 | convolution fusion | flops 1174405120 | bytes 8585216 | tf_op jit(solution)/shard_map/dot_general | solution.py:330
  92.0 2.7 %multiply_convert_fusion = (bf16[320,256]{1,0:T(8,128)(2,1)}, bf16[320,256]{1,0:T(8,128)(2,1)S(1)}, bf16[320,256]{1,0:T(8,128)(2,1)S(1)}, bf16[320]{0:T(512)(128)(2,1)}) fusion(f32[320]{0:T(512)S(1)} %mul.86, f32[320,256]{1,0:T(8,128)S(1)} %fusion.13, f32[2,2,2,40,256]{4,3,2,1,0:T(8,128)S(1)} %copy.83, f32[320,256]{1,0:T(8,128)S(1)} %bitcast.168, ...), kind=kOutput, calls=%fused_computation.40 | convolution fusion | flops 1175961344 | bytes 9734016 | tf_op jit(solution)/shard_map/dot_general | solution.py:330
  94.7 1.4 fusion.11
  96.1 1.4 convolution_add_fusion.2
  97.5 3.6 %convolution_add_fusion.1 = f32[320,7168]{1,0:T(8,128)S(1)} fusion(f32[320,7168]{1,0:T(8,128)S(1)} %convolution_add_fusion.2, bf16[320,256]{1,0:T(8,128)(2,1)S(1)} %bitcast.156, bf16[7168,256]{1,0:T(8,128)(2,1)} %param.21), kind=kOutput, calls=%fused_computation.1 | convolution fusion | flops 1176698880 | bytes 22183936 | tf_op jit(solution)/shard_map/dot_general | solution.py:340
  101.2 1.6 fusion
  103.0 2.4 %pad_maximum_fusion = bf16[320,7296]{1,0:T(8,128)(2,1)} fusion(bf16[320,128]{1,0:T(8,128)(2,1)S(1)} %select_convert_fusion, bf16[320,7168]{1,0:T(8,128)(2,1)S(1)} %fusion), kind=kLoop, calls=%fused_computation.9 | loop fusion | flops 9338880 | bytes 9338880 | tf_op jit(solution)/shard_map/concatenate | solution.py:430
  105.4 0.7 copy.85
  106.1 47.1 %reduce_rows.1 = (bf16[2,8,7296]{2,1,0:T(8,128)(2,1)}, bf16[3,8,7296]{2,1,0:T(8,128)(2,1)}, bf16[3,128,768]{2,1,0:T(8,128)(2,1)}, bf16[7168,256]{1,0:T(8,128)(2,...) custom-call(bf16[8,5,8,7296]{3,2,1,0:T(8,128)(2,1)} %bitcast.136, bf16[320,7168]{1,0:T(8,128)(2,1)} %bitcast.139, ...), custom_call_target="tpu_custom_call" | custom-call | tf_op jit(solution)/shard_map/reduce_rows/pallas_call | solution.py:294
  153.2 1.1 pad_maximum_fusion.4
  154.3 1.8 %constant_dynamic-slice_fusion = (bf16[320,1792]{1,0:T(8,128)(2,1)S(1)}, bf16[320,1792]{1,0:T(8,128)(2,1)S(1)}) fusion(bf16[320,7168]{1,0:T(8,128)(2,1)} %bitcast.147, s32[]{:T(128)S(6)} %select_n.52, bf16[320,7168]{1,0:T(8,128)(2,1)} %bitcast.140), kind=kLoop, calls=%fused_computation.102 | loop fusion | bytes 4587524 | tf_op jit(solution)/shard_map/dynamic_slice | solution.py:440
  156.1 3.1 %convolution_convert_fusion.2 = bf16[1792,256]{1,0:T(8,128)(2,1)} fusion(bf16[384,1792]{1,0:T(8,128)(2,1)} %bitcast.177, bf16[128,1792]{1,0:T(8,128)(2,1)S(1)} %bitcast.167, bf16[512,768]{1,0:T(8,128)(2,1)S(1)} %pad_maximum_fusion.4), kind=kOutput, calls=%fused_computation.25 | convolution fusion | flops 473890816 | bytes 3014656 | tf_op jit(solution)/shard_map/dot_general | solution.py:334
  159.2 1.6 convolution_convert_fusion.3
  160.8 1.6 convolution_convert_fusion.4
  162.8 0.6 fusion.49
  163.4 1.0 fusion.2
  164.3 4.3 %copy.102 = bf16[1,7168,256]{2,1,0:T(8,128)(2,1)} copy(bf16[1,7168,256]{2,1,0:T(8,128)(2,1)} %bitcast.151) | data formatting | bytes 7340032
  168.6 1.9 %copy.103 = bf16[1,7168,256]{2,1,0:T(8,128)(2,1)} copy(bf16[1,7168,256]{2,1,0:T(8,128)(2,1)S(1)} %bitcast.150) | data formatting | bytes 7340032
  170.5 1.5 copy-done.4
  172.0 1.8 %copy.104 = bf16[1,7168,256]{2,1,0:T(8,128)(2,1)} copy(bf16[1,7168,256]{2,1,0:T(8,128)(2,1)S(1)} %bitcast.149) | data formatting | bytes 7340032
  (90 shorter events, 2.8 us)
Async XLA Ops:
  2.9 3.8 %copy-start.17 = (bf16[4,16,128]{2,1,0:T(8,128)(2,1)}, bf16[4,16,128]{2,1,0:T(8,128)(2,1)S(1)}, u32[]{:S(2)}) copy-start(bf16[4,16,128]{2,1,0:T(8,128)(2,1)S(1)} %scatter.9.meta) | copy-start | bytes 49156
  71.5 3.9 %copy-start = (bf16[8,5,8,7168]{3,2,1,0:T(8,128)(2,1)S(1)}, bf16[8,5,8,7168]{3,2,1,0:T(8,128)(2,1)}, u32[]{:S(2)}) copy-start(bf16[8,5,8,7168]{3,2,1,0:T(8,128)(2,1)} %get-tuple-element.45) | copy-start | bytes 13762564
  71.6 6.8 %copy-start.20 = (bf16[7168,256]{1,0:T(8,128)(2,1)S(1)}, bf16[7168,256]{1,0:T(8,128)(2,1)}, u32[]{:S(2)}) copy-start(bf16[7168,256]{1,0:T(8,128)(2,1)} %param.23) | copy-start | bytes 11010052
  75.5 3.8 %copy-start.1 = (bf16[8,5,8,7168]{3,2,1,0:T(8,128)(2,1)S(1)}, bf16[8,5,8,7168]{3,2,1,0:T(8,128)(2,1)}, u32[]{:S(2)}) copy-start(bf16[8,5,8,7168]{3,2,1,0:T(8,128)(2,1)} %get-tuple-element.44) | copy-start | bytes 13762564
  79.2 3.2 %copy-start.18 = (bf16[4,8,16,128]{3,2,1,0:T(8,128)(2,1)S(1)}, bf16[4,8,16,128]{3,2,1,0:T(8,128)(2,1)}, u32[]{:S(2)}) copy-start(bf16[4,8,16,128]{3,2,1,0:T(8,128)(2,1)} %get-tuple-element.43) | copy-start | bytes 393220
  81.6 6.5 %copy-start.9 = (bf16[128,256]{1,0:T(8,128)(2,1)}, bf16[128,256]{1,0:T(8,128)(2,1)S(1)}, u32[]{:S(2)}) copy-start(bf16[128,256]{1,0:T(8,128)(2,1)S(1)} %get-tuple-element.63) | copy-start | bytes 196612
  81.6 6.5 %copy-start.11 = (bf16[128,256]{1,0:T(8,128)(2,1)}, bf16[128,256]{1,0:T(8,128)(2,1)S(1)}, u32[]{:S(2)}) copy-start(bf16[128,256]{1,0:T(8,128)(2,1)S(1)} %get-tuple-element.64) | copy-start | bytes 196612
  81.6 10.3 %slice-start = ((s8[4587520]{0:T(1024)(128)(4,1)}), s8[393216]{0:T(1024)(128)(4,1)S(1)}, s32[]{:S(2)}) async-start(s8[4587520]{0:T(1024)(128)(4,1)} %bitcast.142), calls=%async_computation | async-start | bytes 786432
  83.1 5.0 %copy-start.21 = (bf16[1,7168,256]{2,1,0:T(8,128)(2,1)S(1)}, bf16[1,7168,256]{2,1,0:T(8,128)(2,1)}, u32[]{:S(2)}) copy-start(bf16[1,7168,256]{2,1,0:T(8,128)(2,1)} %param.20) | copy-start | bytes 11010052
  83.1 8.8 %slice-start.1 = ((s8[4587520]{0:T(1024)(128)(4,1)}), s8[4194304]{0:T(1024)(128)(4,1)S(1)}, s32[]{:S(2)}) async-start(s8[4587520]{0:T(1024)(128)(4,1)} %bitcast.142), calls=%async_computation.1 | async-start | bytes 8388608
  88.1 3.9 %copy-start.6 = (bf16[1,7168,256]{2,1,0:T(8,128)(2,1)S(1)}, bf16[1,7168,256]{2,1,0:T(8,128)(2,1)}, u32[]{:S(2)}) copy-start(bf16[1,7168,256]{2,1,0:T(8,128)(2,1)} %param.19) | copy-start | bytes 11010052
  92.0 2.7 %copy-start.2 = (bf16[1,7168,256]{2,1,0:T(8,128)(2,1)S(1)}, bf16[1,7168,256]{2,1,0:T(8,128)(2,1)}, u32[]{:S(2)}) copy-start(bf16[1,7168,256]{2,1,0:T(8,128)(2,1)} %param.18) | copy-start | bytes 11010052
  94.7 1.4 copy-start.8
  94.7 1.4 copy-start.7
  97.5 3.7 %copy-start.14 = (bf16[8,16,256]{2,1,0:T(8,128)(2,1)S(1)}, bf16[8,16,256]{2,1,0:T(8,128)(2,1)}, u32[]{:S(2)}) copy-start(bf16[8,16,256]{2,1,0:T(8,128)(2,1)} %get-tuple-element.60) | copy-start | bytes 196612
  97.5 3.7 %copy-start.3 = (bf16[7168,256]{1,0:T(8,128)(2,1)S(1)}, bf16[7168,256]{1,0:T(8,128)(2,1)}, u32[]{:S(2)}) copy-start(bf16[7168,256]{1,0:T(8,128)(2,1)} %param.22) | copy-start | bytes 11010052
  101.2 1.6 copy-start.19
  102.9 2.4 %copy-start.16 = (bf16[320,256]{1,0:T(8,128)(2,1)S(1)}, bf16[320,256]{1,0:T(8,128)(2,1)}, u32[]{:S(2)}) copy-start(bf16[320,256]{1,0:T(8,128)(2,1)} %get-tuple-element.56) | copy-start | bytes 491524
  106.1 47.1 %copy-start.10 = (bf16[128,256]{1,0:T(8,128)(2,1)S(1)}, bf16[128,256]{1,0:T(8,128)(2,1)}, u32[]{:S(2)}) copy-start(bf16[128,256]{1,0:T(8,128)(2,1)} %copy-done.9) | copy-start | bytes 196612
  106.1 47.1 %copy-start.12 = (bf16[128,256]{1,0:T(8,128)(2,1)S(1)}, bf16[128,256]{1,0:T(8,128)(2,1)}, u32[]{:S(2)}) copy-start(bf16[128,256]{1,0:T(8,128)(2,1)} %copy-done.11) | copy-start | bytes 196612
  156.0 3.1 %copy-start.22 = (bf16[3,8,2,8,1792]{4,3,2,1,0:T(8,128)(2,1)S(1)}, bf16[3,8,2,8,1792]{4,3,2,1,0:T(8,128)(2,1)}, u32[]{:S(2)}) copy-start(bf16[3,8,2,8,1792]{4,3,2,1,0:T(8,128)(2,1)} %get-tuple-element.51) | copy-start | bytes 4128772
  160.8 1.6 copy-start.15
  160.8 1.8 %copy-start.13 = (bf16[3,8,7296]{2,1,0:T(8,128)(2,1)S(1)}, bf16[3,8,7296]{2,1,0:T(8,128)(2,1)}, u32[]{:S(2)}) copy-start(bf16[3,8,7296]{2,1,0:T(8,128)(2,1)} %get-tuple-element.47) | copy-start | bytes 1050628
  164.3 4.3 %copy-start.5 = (bf16[7168,256]{1,0:T(8,128)(2,1)S(1)}, bf16[7168,256]{1,0:T(8,128)(2,1)}, u32[]{:S(2)}) copy-start(bf16[7168,256]{1,0:T(8,128)(2,1)} %get-tuple-element.49) | copy-start | bytes 11010052
  168.6 3.4 %copy-start.4 = (bf16[7168,256]{1,0:T(8,128)(2,1)S(1)}, bf16[7168,256]{1,0:T(8,128)(2,1)}, u32[]{:S(2)}) copy-start(bf16[7168,256]{1,0:T(8,128)(2,1)} %get-tuple-element.50) | copy-start | bytes 11010052
where the time goes:
time: 175 us; the launch traced here: 174 us
  Pallas kernels  112 us (64%)
  matrix products  38.4 us (22%)
  local copies, waits for them, and re-layouts  14.8 us (8%)
  other arithmetic  7.54 us (4%)
    pallas_call x1, Pallas kernels, gather_rows(): pl.pallas_call(functools.partial(gather_kernel, node_count, orders), out_...  64.9 us
    pallas_call x1, Pallas kernels, reduce_rows(): pl.pallas_call(functools.partial(reduce_kernel, node_count, forward, own_...  47.1 us
    dot_general x7, matrix products, dot(): return jnp.dot(left, right, preferred_element_type=jnp.float32)  19.3 us
    unnamed x53, local copies, waits for them, and re-layouts  10.9 us
    dot_general x4, matrix products, contract_last(): lax.dot_general(left, right, (((1,), (1,)), ((), ())), preferred_element_...  8.02 us
    dot_general x3, matrix products, contract_first(): lax.dot_general(left, right, (((0,), (0,)), ((), ())), preferred_element_...  6.29 us

commit v1 on v0

v1 whole, which is shorter than its diff:
```python
import functools

import jax
import jax.numpy as jnp
from jax import lax
from jax.experimental import pallas as pl
from jax.experimental.pallas import tpu as pltpu
from jax.sharding import PartitionSpec as P

E_NODE = 2
LANES = 128
PERM = 64
MESH = pl.DeviceIdType.MESH
GROUPS = 2
BF16, F32, I32 = jnp.bfloat16, jnp.float32, jnp.int32


def masks_of(local_count):
    bits = local_count.bit_length() - 1
    return [1 << b for b in range(1, bits)] + [1]


def near_first(node_count):
    return sorted(range(1, node_count), key=lambda s: min(s, node_count - s))


def dot(left, right):
    return jnp.dot(left, right, preferred_element_type=F32)


def contract_first(left, right):
    return lax.dot_general(left, right, (((0,), (0,)), ((), ())), preferred_element_type=F32)


def contract_last(left, right):
    return lax.dot_general(left, right, (((1,), (1,)), ((), ())), preferred_element_type=F32)


def iota(shape, axis):
    return lax.broadcasted_iota(I32, shape, axis)


def flag(values):
    return jnp.where(values, 1.0, 0.0).astype(F32)


def routing_plan(ids, gates, n, nodes, cap):
    held = ids.shape[0]
    shift = cap.bit_length() - 1
    rest = held - cap
    rows, rest_rows = nodes * cap, nodes * rest
    half = cap // 2
    eye = flag(iota((held, held), 0) == iota((held, held), 1))
    ids_t = contract_first(ids.astype(F32), eye).astype(I32)
    gates_t = contract_first(gates.astype(F32), eye)
    node = ids_t >> 1
    which = ids_t & 1
    rel = node - n
    rel = jnp.where(rel < 0, rel + nodes, rel)
    count = ids.shape[1]
    lane_node = iota((nodes, held), 0)
    hit = jnp.zeros((nodes, held), F32)
    gate_of = [jnp.zeros((nodes, held), F32) for _ in range(E_NODE)]
    for k in range(count):
        here = lane_node == rel[k : k + 1, :]
        hit = jnp.maximum(hit, flag(here))
        for e in range(E_NODE):
            named = here & (which[k : k + 1, :] == e)
            gate_of[e] = gate_of[e] + jnp.where(named, gates_t[k : k + 1, :], 0.0)
    upper = flag(iota((held, held), 0) <= iota((held, held), 1))
    rank = dot(hit, upper) - 1.0
    spread = flag((iota((rows, nodes), 0) >> shift) == iota((rows, nodes), 1))
    slot = (iota((rows, held), 0) & (cap - 1)).astype(F32)
    first = flag((dot(spread, hit) > 0.5) & (dot(spread, rank) == slot))

    row, lane = iota((rows, rows), 0), iota((rows, rows), 1)
    unit = flag(row == lane)
    ends = contract_last(first, first) * (1.0 - unit)
    pairs = flag((row ^ 1) == lane)
    reach = unit + dot(ends, pairs)
    for _ in range((held - 1).bit_length()):
        reach = jnp.minimum(dot(reach, reach), 1.0)
    number = lane.astype(F32)
    far = dot(ends, reach)
    label = jnp.min(jnp.where(reach > 0.5, number, float(rows)), axis=1, keepdims=True)
    other = jnp.min(jnp.where(far > 0.5, number, float(rows)), axis=1, keepdims=True)
    taken = flag(label < other)
    same = (row >> shift) == (lane >> shift)
    before = flag(same & (lane < row))
    taken_wide = jnp.broadcast_to(taken, (rows, LANES))
    taken_rank = dot(before, taken_wide)[:, 0:1]
    left_rank = dot(before, 1.0 - taken_wide)[:, 0:1]
    place = jnp.where(taken > 0.5, taken_rank, left_rank + float(half))
    move = flag(same & (place == (lane & (cap - 1)).astype(F32)))
    pick = contract_first(move, first)

    assigned = pick * flag((iota((rows, held), 0) & (cap - 1)) < half)
    weights = [
        jnp.sum(pick * dot(spread, gate_of[e]), axis=1, keepdims=True) for e in range(E_NODE)
    ]
    spot = flag(iota((rows, LANES), 1) == iota((rows, LANES), 0) + PERM)
    lanes = iota((rows, LANES), 1)
    meta = dot(contract_last(pick, assigned), spot)
    for e in range(E_NODE):
        meta = meta + jnp.where(lanes == e, weights[e], 0.0)

    shape = (rest_rows, held)
    block = jnp.zeros(shape, I32)
    for r in range(1, nodes):
        block = block + jnp.where(iota(shape, 0) >= r * rest, 1, 0)
    within = (iota(shape, 0) - block * rest).astype(F32)
    spread_rest = flag(block[:, 0:1] == iota((rest_rows, nodes), 1))
    away = 1.0 - hit
    away_rank = dot(away, upper) - 1.0
    absent = flag((dot(spread_rest, away) > 0.5) & (dot(spread_rest, away_rank) == within))
    meta_rest = dot(contract_last(absent, assigned), spot)
    return pick, meta, absent, meta_rest


def silu_parts(pre_gate):
    sig = jax.nn.sigmoid(pre_gate)
    return (pre_gate * sig, sig * (1.0 + pre_gate * (1.0 - sig)))


def ffn_backward(pre_gate, pre_up, upstream, weight):
    activ, slope = silu_parts(pre_gate)
    hidden = activ * pre_up
    scaled = weight * upstream
    grad_up = (scaled * activ).astype(BF16)
    grad_gate = (scaled * pre_up * slope).astype(BF16)
    weighted = (weight * hidden).astype(BF16)
    return (grad_gate, grad_up, weighted, hidden * upstream)


def main_kernel(
    nodes, local_count, cap,
    tok, grad, ids, gates, w0, w1, w2, w3, w4, w5,
    rows_out, grads_out, packs, ext, back, pick_out,
    rows, away, mine, wbuf, part, land, pre, packed,
    send_sem, recv_sem, copy_sem,
):
    n, l = lax.axis_index("node"), lax.axis_index("local")
    held, width = tok.shape
    units = w0.shape[1]
    piece = width // nodes
    masks = masks_of(local_count)
    bits = len(masks)
    rest = held - cap
    half = cap // 2
    order = near_first(nodes)
    items = [0] + order
    span = nodes // GROUPS
    total = span * local_count * cap
    copies = []
    sends = []

    def local_copy(src, dst):
        copy = pltpu.make_async_copy(src, dst, copy_sem.at[len(copies)])
        copy.start()
        copies.append(copy)
        return copy

    def remote(src, dst, device):
        i = len(sends)
        copy = pltpu.make_async_remote_copy(
            src_ref=src, dst_ref=dst, send_sem=send_sem.at[i], recv_sem=recv_sem.at[i],
            device_id=device, device_id_type=MESH,
        )
        copy.start()
        sends.append(copy)
        return copy

    loads = [local_copy(w, wbuf.at[i]) for i, w in enumerate((w0, w1, w2, w3, w4, w5))]

    barrier = pltpu.get_barrier_semaphore()
    for r in range(1, nodes):
        pl.semaphore_signal(
            barrier, inc=1, device_id=(lax.rem(n + r, nodes), l), device_id_type=MESH
        )
    for mask in masks:
        pl.semaphore_signal(barrier, inc=1, device_id=(n, l ^ mask), device_id_type=MESH)

    pick, meta, absent, meta_rest = routing_plan(ids[...], gates[...], n, nodes, cap)
    pick_out[...] = pick.astype(BF16)
    pick_b, absent_b = pick.astype(BF16), absent.astype(BF16)

    def place(r, columns, values):
        if r == 0:
            rows[0, 0, :, columns] = values
        else:
            away[r - 1, :, columns] = values

    tile = width // 7
    for source, base in ((tok, 0), (grad, width)):
        for c in range(7):
            chosen = dot(pick_b, source[:, c * tile : (c + 1) * tile])
            for r in range(nodes):
                place(
                    r, pl.ds(base + c * tile, tile),
                    chosen[r * cap : (r + 1) * cap].astype(BF16),
                )
    for r in range(nodes):
        place(r, pl.ds(2 * width, LANES), meta[r * cap : (r + 1) * cap].astype(BF16))
        start = pl.multiple_of(lax.rem(n + r, nodes) * piece, LANES)
        these = absent_b[r * rest : (r + 1) * rest]
        mine[r, :, 0:piece] = dot(these, tok[:, pl.ds(start, piece)]).astype(BF16)
        mine[r, :, piece : 2 * piece] = dot(these, grad[:, pl.ds(start, piece)]).astype(BF16)
        mine[r, :, 2 * piece :] = meta_rest[r * rest : (r + 1) * rest].astype(BF16)

    pl.semaphore_wait(barrier, nodes - 1 + bits)

    arrived = {}
    buffers = {"rows": (rows, width), "ext": (ext, piece)}

    def pass_on(name, k, p, columns):
        buf, _ = buffers[name]
        for b in range(2, bits):
            if p < 1 << b:
                q = p + (1 << b)
                arrived.setdefault((name, k, q), []).append((columns, remote(
                    buf.at[k, p, :, columns], buf.at[k, q, :, columns], (n, l ^ masks[b])
                )))

    def own(name, k):
        buf, _ = buffers[name]
        for b in range(2):
            arrived[name, k, 1 << b] = [(None, remote(
                buf.at[k, 0], buf.at[k, 1 << b], (n, l ^ masks[b])
            ))]
        pass_on(name, k, 0, slice(None))

    def forward(name, k):
        buf, split = buffers[name]
        ends = buf.shape[-1]
        parts = (pl.ds(0, split), pl.ds(split, ends - split))
        for p, over in ((1, 1), (2, 0)):
            for _, copy in arrived[name, k, p]:
                copy.wait_recv()
            columns = parts[p - 1]
            arrived.setdefault((name, k, 3), []).append((columns, remote(
                buf.at[k, p, :, columns], buf.at[k, 3, :, columns], (n, l ^ masks[over])
            )))
            pass_on(name, k, p, slice(None))

    def corner(name, k):
        for p in range(3, local_count // 2):
            for columns, copy in list(arrived[name, k, p]):
                copy.wait_recv()
                pass_on(name, k, p, columns)

    def complete(name, k):
        for p in range(local_count // 2, local_count):
            for _, copy in arrived[name, k, p]:
                copy.wait_recv()

    entering = {}
    own("rows", 0)
    for s in order:
        entering["rows", s] = remote(
            away.at[nodes - s - 1], rows.at[items.index(s), 0],
            (lax.rem(n + nodes - s, nodes), l),
        )
    for s in order:
        entering["ext", s] = remote(
            mine.at[nodes - s], ext.at[items.index(s), 0], (lax.rem(n + nodes - s, nodes), l)
        )
    ext_own = local_copy(mine.at[0], ext.at[0, 0])

    def enter(name, k):
        entering[name, items[k]].wait_recv()
        own(name, k)

    expert = l // (local_count // E_NODE)
    slots = iota((total, 1), 0) & (cap - 1)
    is_shared = flag(slots < half)
    deep = width // 7

    def chunk(g, columns):
        return rows[g * span : (g + 1) * span, :, :, columns].reshape(total, -1)

    def ffn(g):
        for i in range(6):
            pre[i] = jnp.zeros((total, units), F32)

        def step(c, carry):
            at = pl.multiple_of(c * deep, LANES)
            left_t = chunk(g, pl.ds(at, deep))
            left_g = chunk(g, pl.ds(width + at, deep))
            for i, left in enumerate((left_t, left_t, left_g) * 2):
                pre[i] += dot(left, wbuf[i, pl.ds(at, deep), :])
            return carry

        lax.fori_loop(0, 7, step, 0)
        table = chunk(g, pl.ds(2 * width, LANES)).astype(F32)
        weight = jnp.where(expert == 0, table[:, 0:1], table[:, 1:2])
        gg, gu, gh, product = ffn_backward(pre[0], pre[1], pre[2], weight)
        sg, su, sh, _ = ffn_backward(pre[3], pre[4], pre[5], is_shared)
        span_rows = pl.ds(g * total, total)
        for i, value in enumerate((gg, gu, gh)):
            grads_out[span_rows, i * units : (i + 1) * units] = value
        score = jnp.sum(product, axis=1, keepdims=True)
        lanes = iota((total, LANES), 1)
        score = jnp.where(lanes == expert, score, 0.0)
        part[g * span : (g + 1) * span, :, :, width:] = score.reshape(
            span, local_count, cap, LANES
        ).astype(BF16)
        kept = total * half // cap
        shift, low = cap.bit_length() - 1, half.bit_length() - 1
        j, h = iota((kept, total), 0), iota((kept, total), 1)
        compact = flag(h == ((j >> low) << shift) + (j & (half - 1))).astype(BF16)
        for i, value in enumerate((sg, su, sh)):
            packed[g, :, i * units : (i + 1) * units] = dot(compact, value).astype(BF16)
        return (gg, gu, sg, su)

    def spread_dx(g, values):
        gg, gu, sg, su = values

        def step(c, carry):
            at = pl.multiple_of(c * deep, LANES)
            for sub in range(2):
                size = deep // 2
                cols = pl.ds(pl.multiple_of(at + sub * size, LANES), size)
                total_dx = (
                    contract_last(gg, wbuf[0, cols, :]) + contract_last(gu, wbuf[1, cols, :])
                    + contract_last(sg, wbuf[3, cols, :]) + contract_last(su, wbuf[4, cols, :])
                )
                part[g * span : (g + 1) * span, :, :, cols] = total_dx.reshape(
                    span, local_count, cap, size
                ).astype(BF16)
            return carry

        lax.fori_loop(0, 7, step, 0)

    def send_packs(g):
        local_copy(packed.at[g], packs.at[0, g])
        for r in range(1, nodes):
            waits.append(remote(
                packed.at[g], packs.at[nodes - r, g], (lax.rem(n + r, nodes), l)
            ))

    waits = []
    full = part.shape[-1]
    cut = width // 2
    sides = (pl.ds(0, cut), pl.ds(cut, full - cut))
    everything = pl.ds(0, full)
    flight = {}
    upper = bits - 2

    def moves(stage):
        if stage < upper:
            b = bits - 1 - stage
            return [(1 << b, 1 << b, everything, masks[b], 1 << b)]
        if stage == upper:
            return [
                (1, 1, sides[0], masks[0], 1), (3, 1, sides[0], masks[0], 1),
                (2, 2, sides[1], masks[1], 2),
            ]
        return [(2, 1, sides[0], masks[1], 2), (1, 1, sides[1], masks[0], 1)]

    def reduce_start(g, stage):
        for k in range(g * span, (g + 1) * span):
            flight[k, stage] = [
                remote(
                    part.at[k, pl.ds(p, size), :, columns],
                    land.at[k, pl.ds(p, size), :, columns], (n, l ^ mask),
                )
                for p, size, columns, mask, _ in moves(stage)
            ]

    def reduce_settle(g, stage):
        for k in range(g * span, (g + 1) * span):
            for (p, size, columns, _, gap), copy in zip(moves(stage), flight[k, stage]):
                copy.wait_recv()

                def add(i, carry, k=k, p=p, gap=gap, columns=columns):
                    there = land[k, p + i, :, columns].astype(F32)
                    here = part[k, p + i - gap, :, columns].astype(F32)
                    part[k, p + i - gap, :, columns] = (here + there).astype(BF16)
                    return carry

                lax.fori_loop(0, size, add, 0)

    def go_home(g):
        for k in range(g * span, (g + 1) * span):
            s = items[k]
            if s == 0:
                local_copy(part.at[k, 0], back.at[0])
            else:
                waits.append(remote(
                    part.at[k, 0], back.at[nodes - s], (lax.rem(n + s, nodes), l)
                ))

    for k in range(nodes):
        if k > 0:
            enter("rows", k)
            forward("rows", k - 1)
        if k > 1:
            corner("rows", k - 2)
    for load in loads:
        load.wait()
    for k in range(span):
        if k == nodes - 2:
            corner("rows", k)
        complete("rows", k)
    values = ffn(0)
    send_packs(0)
    forward("rows", nodes - 1)
    corner("rows", nodes - 2)
    spread_dx(0, values)
    corner("rows", nodes - 1)
    reduce_start(0, 0)
    ext_own.wait()
    own("ext", 0)
    for k in range(1, nodes):
        enter("ext", k)
    for k in range(span, nodes):
        complete("rows", k)
    for k in range(nodes):
        local_copy(rows.at[k], rows_out.at[k])
    values = ffn(1)
    send_packs(1)
    reduce_settle(0, 0)
    reduce_start(0, 1)
    spread_dx(1, values)
    reduce_start(1, 0)
    for k in range(nodes):
        forward("ext", k)
    for stage in range(1, upper + 2):
        reduce_settle(0, stage)
        if stage < upper + 1:
            reduce_start(0, stage + 1)
        reduce_settle(1, stage - 1)
        reduce_start(1, stage)
    go_home(0)
    for k in range(nodes):
        corner("ext", k)
    reduce_settle(1, upper + 1)
    go_home(1)
    for k in range(nodes):
        complete("ext", k)
    for copy in waits:
        copy.wait_recv()
    for copy in copies[len(loads):]:
        if copy is not ext_own:
            copy.wait()
    for copy in sends:
        copy.wait_send()


def main_call(nodes, local_count, cap, tok, grad, ids, gates, weights):
    held, width = tok.shape
    units = weights[0].shape[1]
    rest, piece = held - cap, width // nodes
    span = nodes // GROUPS
    total = span * local_count * cap
    kept = total // 2
    full, wide, narrow = width + LANES, 2 * width + LANES, 2 * piece + LANES
    vmem = pl.BlockSpec(memory_space=pltpu.VMEM)
    hbm = pl.BlockSpec(memory_space=pl.ANY)
    shape = jax.ShapeDtypeStruct
    bits = local_count.bit_length() - 1
    gathers = 4
    for b in range(2, bits):
        gathers += (1 << b) + 1 + (b - 2) * 2
    gathers = 4 + sum(5 * 2 ** (b - 2) for b in range(2, bits))
    reduces = (bits - 2) + 5
    count = nodes * (2 * gathers + reduces) + (nodes - 1) * (3 + GROUPS)
    return pl.pallas_call(
        functools.partial(main_kernel, nodes, local_count, cap),
        out_shape=[
            shape((nodes, local_count, cap, wide), BF16),
            shape((nodes * local_count * cap, 3 * units), BF16),
            shape((nodes, GROUPS, kept, 3 * units), BF16),
            shape((nodes, local_count, rest, narrow), BF16),
            shape((nodes, cap, full), BF16),
            shape((nodes * cap, held), BF16),
        ],
        in_specs=[vmem] * 4 + [hbm] * 6,
        out_specs=[hbm, vmem, hbm, hbm, hbm, vmem],
        scratch_shapes=[
            pltpu.VMEM((nodes, local_count, cap, wide), BF16),
            pltpu.VMEM((nodes - 1, cap, wide), BF16),
            pltpu.VMEM((nodes, rest, narrow), BF16),
            pltpu.VMEM((6, width, units), BF16),
            pltpu.VMEM((nodes, local_count, cap, full), BF16),
            pltpu.VMEM((nodes, local_count, cap, full), BF16),
            pltpu.VMEM((6, total, units), F32),
            pltpu.VMEM((GROUPS, kept, 3 * units), BF16),
            pltpu.SemaphoreType.DMA((count,)),
            pltpu.SemaphoreType.DMA((count,)),
            pltpu.SemaphoreType.DMA((6 + 1 + GROUPS + nodes + 1,)),
        ],
        compiler_params=pltpu.CompilerParams(
            collective_id=0, has_side_effects=True, vmem_limit_bytes=67043328
        ),
        name="exchange",
    )(tok, grad, ids, gates, *weights)


def finish_kernel(
    nodes, local_count, cap, rest, order,
    where_ref, t_rows, g_rows, r_meta, t_piece, g_piece, t_ext, g_ext, e_meta,
    grads, packs, back, score, pick, ids,
    dw_g, dw_u, dw_d, ds_g, ds_u, ds_d, dx, dgates,
    near, far,
):
    units = dw_g.shape[1]
    half = cap // 2
    rows = nodes * cap
    seats = local_count * half
    items = [0] + order
    step = pl.program_id(0)

    @pl.when(step == 0)
    def _():
        shift, low = cap.bit_length() - 1, half.bit_length() - 1
        columns = nodes * seats
        seat = local_count.bit_length() - 1 + low
        h, j = iota((rows, columns), 0), iota((rows, columns), 1)
        widen = flag(
            ((h >> shift) == (j >> seat)) & ((h & (cap - 1)) == (j & (half - 1)))
        ).astype(BF16)
        block_of = (iota((1, columns), 1) & (seats - 1)) >> low
        for k, s in enumerate(items):
            pieces = []
            for r in range(nodes):
                at = (((s + r) % nodes) * nodes + items.index((nodes - r) % nodes)) * seats
                pieces.append(packs[at : at + seats, :])
            table = jnp.concatenate(pieces, axis=0)
            for meta, out, size in ((r_meta, near, cap), (e_meta, far, rest)):
                height = local_count * size
                perm = meta[k * height : (k + 1) * height, PERM : PERM + rows]
                owner = jnp.zeros((height, 1), I32)
                for p in range(1, local_count):
                    owner = owner + jnp.where(iota((height, 1), 0) >= p * size, 1, 0)
                full = jnp.where(owner == block_of, dot(perm, widen), 0.0).astype(BF16)
                out[k * height : (k + 1) * height, :] = dot(full, table).astype(BF16)
        n = where_ref[0]
        pick_t = contract_first(
            pick[...], flag(iota((rows, rows), 0) == iota((rows, rows), 1)).astype(BF16)
        )
        held = pick_t.shape[0]
        total = jnp.zeros((held, dgates.shape[1]), F32)
        rel = (ids[...] >> 1) - n
        rel = jnp.where(rel < 0, rel + nodes, rel)
        which = ids[...] & 1
        for k in range(dgates.shape[1]):
            here = (iota((held, rows), 1) >> shift) == rel[:, k : k + 1]
            found = dot(jnp.where(here, pick_t, 0.0).astype(BF16), score[...])
            found = jnp.where(iota((held, LANES), 1) == which[:, k : k + 1], found, 0.0)
            value = jnp.sum(found, axis=1, keepdims=True)
            total = jnp.where(iota((held, dgates.shape[1]), 1) == k, value, total)
        dgates[...] = total

    t, g = t_rows[...], g_rows[...]
    dw_g[...] = contract_first(t, grads[:, 0:units]).astype(BF16)
    dw_u[...] = contract_first(t, grads[:, units : 2 * units]).astype(BF16)
    dw_d[...] = contract_first(g, grads[:, 2 * units :]).astype(BF16)
    t_near, g_near, t_far, g_far = t_piece[...], g_piece[...], t_ext[...], g_ext[...]
    for i, (out, a, b) in enumerate((
        (ds_g, t_near, t_far), (ds_u, t_near, t_far), (ds_d, g_near, g_far),
    )):
        cols = slice(i * units, (i + 1) * units)
        out[...] = (contract_first(a, near[:, cols]) + contract_first(b, far[:, cols])).astype(
            BF16
        )
    dx[...] = contract_first(pick[...], back[...]).astype(BF16)


def finish_call(nodes, local_count, cap, n, rows, ext, grads, packs, back, pick, ids, width):
    units = grads.shape[1] // 3
    held = ids.shape[0]
    rest, piece = held - cap, width // nodes
    count = nodes * local_count * cap
    far_count = nodes * local_count * rest
    slots = nodes * cap
    blocks = piece // LANES
    steps = blocks // 2 if blocks % 2 == 0 else blocks
    tile, slim = width // steps, piece // steps
    rows = rows.reshape(count, -1)
    ext = ext.reshape(far_count, -1)
    back = back.reshape(slots, -1)
    packs = packs.reshape(-1, packs.shape[-1])

    def whole(shape):
        return pl.BlockSpec(shape, lambda j, n: (0,) * len(shape))

    def band(height, size, start):
        return pl.BlockSpec((height, size), lambda j, n: (0, start + j))

    def fixed(height, at):
        return pl.BlockSpec((height, LANES), lambda j, n: (0, at))

    def here(start):
        return pl.BlockSpec((count, slim), lambda j, n: (0, start + n[0] * steps + j))

    def out_rows(size):
        return pl.BlockSpec((size, units), lambda j, n: (j, 0))

    shape = jax.ShapeDtypeStruct
    flops = 2 * count * width * units * 3 + 2 * (count + far_count) * piece * units * 3
    return pl.pallas_call(
        functools.partial(finish_kernel, nodes, local_count, cap, rest, near_first(nodes)),
        grid_spec=pltpu.PrefetchScalarGridSpec(
            num_scalar_prefetch=1,
            grid=(steps,),
            in_specs=[
                band(count, tile, 0), band(count, tile, steps), fixed(count, 2 * width // LANES),
                here(0), here(width // slim),
                band(far_count, slim, 0), band(far_count, slim, steps),
                fixed(far_count, 2 * piece // LANES),
                whole(grads.shape), whole(packs.shape),
                band(slots, tile, 0), fixed(slots, width // LANES),
                whole(pick.shape), whole(ids.shape),
            ],
            out_specs=[out_rows(tile)] * 3 + [out_rows(slim)] * 3 + [
                pl.BlockSpec((held, tile), lambda j, n: (0, j)), whole(ids.shape),
            ],
            scratch_shapes=[
                pltpu.VMEM((count, 3 * units), BF16),
                pltpu.VMEM((far_count, 3 * units), BF16),
            ],
        ),
        out_shape=[shape((width, units), BF16)] * 3 + [shape((piece, units), BF16)] * 3 + [
            shape((held, width), BF16), shape(ids.shape, F32),
        ],
        cost_estimate=pl.CostEstimate(
            flops=flops, bytes_accessed=2 * (rows.size + 3 * width * units), transcendentals=0
        ),
        name="finish",
    )(n, rows, rows, rows, rows, rows, ext, ext, ext, grads, packs, back, back, pick, ids)


def local(tokens, grad_out, gates, expert_ids, w_gate, w_up, w_down, s_gate, s_up, s_down):
    held, width = tokens.shape
    nodes, locals_ = lax.axis_size("node"), lax.axis_size("local")
    cap = 2 * held // nodes
    weights = (w_gate[0], w_up[0], w_down[0], s_gate, s_up, s_down)
    rows, grads, packs, ext, back, pick = main_call(
        nodes, locals_, cap, tokens, grad_out, expert_ids, gates, weights
    )
    n = lax.axis_index("node").astype(I32).reshape(1)
    dw_g, dw_u, dw_d, ds_g, ds_u, ds_d, dx, dgates = finish_call(
        nodes, locals_, cap, n, rows, ext, grads, packs, back, pick, expert_ids, width
    )
    return (dx, dgates, dw_g[None], dw_u[None], dw_d[None], ds_g, ds_u, ds_d)


def solution(mesh):
    token = P(("node", "local"), None)
    routed = P("node", None, "local")
    shared = P(None, "local")
    shared_out = P("node", "local")
    return jax.shard_map(
        local,
        mesh=mesh,
        in_specs=(token,) * 4 + (routed,) * 3 + (shared,) * 3,
        out_specs=(token,) * 2 + (routed,) * 3 + (shared_out,) * 3,
        check_vma=False,
    )
```

time: 175 us -> 105 us (0.60)
  matrix products: 38.4 us -> 0 us
  Pallas kernels: 112 us -> 100 us
  local copies, waits for them, and re-layouts: 14.8 us -> 4.06 us
  other arithmetic: 7.54 us -> 0 us
    dot_general x17 -> x0, matrix products: 38.4 us -> none  [the longest x7 19.3 us: dot(): return jnp.dot(left, right, preferred_element_type=jnp.float32)]
    pallas_call x2, Pallas kernels: 112 us -> 100 us  [the longest x1 84.9 us: main_call(): pl.pallas_call(functools.partial(main_kernel, nodes, local_count, cap), o...]
    unnamed x53 -> x3, local copies, waits for them, and re-layouts: 10.9 us -> 4.06 us
    concatenate x4 -> x0, other arithmetic: 4.25 us -> none  [the longest x1 2.43 us: local(): jnp.concatenate([partial_dx, score], axis=1)]
    dynamic_slice x1 -> x0, local copies, waits for them, and re-layouts: 1.76 us -> none  [local(): here_g = own(lax.dynamic_slice_in_dim(rows_g, start, piece, 1))]
where the time goes in v1:
time: 105 us
  Pallas kernels  100 us (95%)
  local copies, waits for them, and re-layouts  4.06 us (4%)
    pallas_call x1, Pallas kernels, main_call(): pl.pallas_call(functools.partial(main_kernel, nodes, local_count, cap), o...  84.9 us
    pallas_call x1, Pallas kernels, finish_call(): pl.pallas_call(functools.partial(finish_kernel, nodes, local_count, cap,...  15.2 us
    unnamed x3, local copies, waits for them, and re-layouts  4.06 us

profile of v1, /device:TPU:0, one launch (start us, length us, event | category | flops | bytes accessed | tf_op | source)
XLA Modules:
  0.0 104.7 jit_solution(2501539323157785942)
XLA Ops:
  0.6 1.4 %copy.19.gates = bf16[16,3]{1,0:T(8,128)(2,1)} copy(bf16[16,3]{0,1:T(4,128)(2,1)} %param.12) | data formatting | bytes 192 | tf_op args[2]
  2.0 1.4 %copy.18.ids = s32[16,3]{1,0:T(8,128)} copy(s32[16,3]{0,1:T(4,128)} %param.13) | data formatting | bytes 384 | tf_op args[3]
  3.3 84.9 %exchange.1 = (bf16[4,8,8,14464]{3,2,1,0:T(8,128)(2,1)}, bf16[256,768]{1,0:T(8,128)(2,1)}, bf16[4,2,64,768]{3,2,1,0:T(8,128)(2,1)}, bf16[4,8,8,3712]{3,2,1,0:T(8...) custom-call(bf16[16,7168]{1,0:T(8,128)(2,1)} %tok.1, bf16[16,7168]{1,0:T(8,128)(2,1)} %grad.1, ...), custom_call_target="tpu_custom_call" | custom-call | tf_op jit(solution)/shard_map/exchange/pallas_call | solution.py:468
  88.2 15.2 %finish.1 = (bf16[7168,256]{1,0:T(8,128)(2,1)}, bf16[7168,256]{1,0:T(8,128)(2,1)}, bf16[7168,256]{1,0:T(8,128)(2,1)}, bf16[1792,256]{1,0:T(8,128)(2,1)}, bf16[17...) custom-call(s32[1]{0:T(128)} %bitcast.where_ref, ...), custom_call_target="tpu_custom_call" | custom-call | flops 4227858432 | bytes 18415616 | tf_op jit(solution)/shard_map/finish/pallas_call | solution.py:602
  103.4 1.3 %copy.21 = f32[16,3]{0,1:T(4,128)} copy(f32[16,3]{1,0:T(8,128)} %get-tuple-element.37) | data formatting | bytes 384

commit v2 on v1

v2 whole, which is shorter than its diff:
```python
import functools
import math

import jax
import jax.numpy as jnp
from jax import lax
from jax.experimental import pallas as pl
from jax.experimental.pallas import tpu as pltpu
from jax.sharding import PartitionSpec as P

E_NODE = 2
LANES = 128
PERM = 64
MESH = pl.DeviceIdType.MESH
BF16, F32, I32 = jnp.bfloat16, jnp.float32, jnp.int32


def masks_of(local_count):
    bits = local_count.bit_length() - 1
    return [1 << b for b in range(1, bits)] + [1]


def order_of(node_count):
    return [0, 2, 1, 3] if node_count == 4 else list(range(node_count))


def spans_of(node_count):
    return [(0, node_count // 2), (node_count // 2, node_count - node_count // 2)]


def dot(left, right):
    return jnp.dot(left, right, preferred_element_type=F32)


def contract_first(left, right):
    return lax.dot_general(left, right, (((0,), (0,)), ((), ())), preferred_element_type=F32)


def contract_last(left, right):
    return lax.dot_general(left, right, (((1,), (1,)), ((), ())), preferred_element_type=F32)


def iota(shape, axis):
    return lax.broadcasted_iota(I32, shape, axis)


def flag(values):
    return jnp.where(values, 1.0, 0.0).astype(F32)


def routing_plan(ids, gates, n, nodes, cap):
    held = ids.shape[1]
    shift = cap.bit_length() - 1
    rest = held - cap
    rows, rest_rows = nodes * cap, nodes * rest
    half = cap // 2
    gates = gates.astype(F32)
    rel = (ids >> 1) ^ n
    which = ids & 1
    count = ids.shape[0]
    lane_node = iota((nodes, held), 0)
    hit = jnp.zeros((nodes, held), F32)
    gate_of = [jnp.zeros((nodes, held), F32) for _ in range(E_NODE)]
    for k in range(count):
        here = lane_node == rel[k : k + 1, :]
        hit = jnp.maximum(hit, flag(here))
        for e in range(E_NODE):
            named = here & (which[k : k + 1, :] == e)
            gate_of[e] = gate_of[e] + jnp.where(named, gates[k : k + 1, :], 0.0)
    upper = flag(iota((held, held), 0) <= iota((held, held), 1))
    rank = dot(hit, upper) - 1.0
    spread = flag((iota((rows, nodes), 0) >> shift) == iota((rows, nodes), 1))
    slot = (iota((rows, held), 0) & (cap - 1)).astype(F32)
    first = flag((dot(spread, hit) > 0.5) & (dot(spread, rank) == slot))

    row, lane = iota((rows, rows), 0), iota((rows, rows), 1)
    unit = flag(row == lane)
    ends = contract_last(first, first) * (1.0 - unit)
    pairs = flag((row ^ 1) == lane)
    reach = unit + dot(ends, pairs)
    for _ in range((held - 1).bit_length()):
        reach = jnp.minimum(dot(reach, reach), 1.0)
    number = lane.astype(F32)
    far = dot(ends, reach)
    label = jnp.min(jnp.where(reach > 0.5, number, float(rows)), axis=1, keepdims=True)
    other = jnp.min(jnp.where(far > 0.5, number, float(rows)), axis=1, keepdims=True)
    taken = flag(label < other)
    same = (row >> shift) == (lane >> shift)
    before = flag(same & (lane < row))
    taken_wide = jnp.broadcast_to(taken, (rows, LANES))
    taken_rank = dot(before, taken_wide)[:, 0:1]
    left_rank = dot(before, 1.0 - taken_wide)[:, 0:1]
    place = jnp.where(taken > 0.5, taken_rank, left_rank + float(half))
    move = flag(same & (place == (lane & (cap - 1)).astype(F32)))
    pick = contract_first(move, first)

    assigned = pick * flag((iota((rows, held), 0) & (cap - 1)) < half)
    weights = [
        jnp.sum(pick * dot(spread, gate_of[e]), axis=1, keepdims=True) for e in range(E_NODE)
    ]
    spot = flag(iota((rows, LANES), 1) == iota((rows, LANES), 0) + PERM)
    lanes = iota((rows, LANES), 1)
    meta = dot(contract_last(pick, assigned), spot)
    for e in range(E_NODE):
        meta = meta + jnp.where(lanes == e, weights[e], 0.0)

    shape = (rest_rows, held)
    block = jnp.zeros(shape, I32)
    for r in range(1, nodes):
        block = block + jnp.where(iota(shape, 0) >= r * rest, 1, 0)
    within = (iota(shape, 0) - block * rest).astype(F32)
    spread_rest = flag(block[:, 0:1] == iota((rest_rows, nodes), 1))
    away = 1.0 - hit
    away_rank = dot(away, upper) - 1.0
    absent = flag((dot(spread_rest, away) > 0.5) & (dot(spread_rest, away_rank) == within))
    meta_rest = dot(contract_last(absent, assigned), spot)
    return pick, meta, absent, meta_rest


def silu_parts(pre_gate):
    sig = jax.nn.sigmoid(pre_gate)
    return (pre_gate * sig, sig * (1.0 + pre_gate * (1.0 - sig)))


def ffn_backward(pre_gate, pre_up, upstream, weight):
    activ, slope = silu_parts(pre_gate)
    hidden = activ * pre_up
    scaled = weight * upstream
    grad_up = (scaled * activ).astype(BF16)
    grad_gate = (scaled * pre_up * slope).astype(BF16)
    weighted = (weight * hidden).astype(BF16)
    return (grad_gate, grad_up, weighted, hidden * upstream)


def main_kernel(
    nodes, local_count, cap,
    tok, grad, ids, gates, w0, w1, w2, w3, w4, w5,
    rows, ext, near, far, dw_g, dw_u, dw_d, back, pick_out,
    packs, away, mine, w_in, w_out, turned, part, land, pre, grads,
    send_sem, recv_sem, cross_send, cross_recv, load_sem,
):
    n, l = lax.axis_index("node"), lax.axis_index("local")
    held, width = tok.shape
    units = w0.shape[1]
    piece = width // nodes
    masks = masks_of(local_count)
    bits = len(masks)
    rest = held - cap
    half = cap // 2
    seats = local_count * half
    spans = spans_of(nodes)
    order = order_of(nodes)
    sends = []

    def remote(src, dst, device):
        i = len(sends)
        copy = pltpu.make_async_remote_copy(
            src_ref=src, dst_ref=dst, send_sem=send_sem.at[i], recv_sem=recv_sem.at[i],
            device_id=device, device_id_type=MESH,
        )
        copy.start()
        sends.append(copy)
        return copy

    barrier = pltpu.get_barrier_semaphore()
    for r in range(1, nodes):
        pl.semaphore_signal(barrier, inc=1, device_id=(n ^ r, l), device_id_type=MESH)
    for mask in masks:
        pl.semaphore_signal(barrier, inc=1, device_id=(n, l ^ mask), device_id_type=MESH)

    loads = []
    stack = ((w0, w_in, 0), (w1, w_in, 1), (w3, w_in, 2), (w4, w_in, 3), (w2, w_out, 0), (w5, w_out, 1))
    for i, (w, buf, at) in enumerate(stack):
        load = pltpu.make_async_copy(w, buf.at[:, at * units : (at + 1) * units], load_sem.at[i])
        load.start()
        loads.append(load)

    pick, meta, absent, meta_rest = routing_plan(ids[...], gates[...], n, nodes, cap)
    pick_out[...] = pick.astype(BF16)
    pick_b, absent_b = pick.astype(BF16), absent.astype(BF16)

    def place(r, columns, values):
        if r == 0:
            rows[0, 0, :, columns] = values
        else:
            away[r - 1, :, columns] = values

    tile = width // 7
    for source, base in ((tok, 0), (grad, width)):
        for c in range(7):
            chosen = dot(pick_b, source[:, c * tile : (c + 1) * tile])
            for r in range(nodes):
                place(
                    r, pl.ds(base + c * tile, tile),
                    chosen[r * cap : (r + 1) * cap].astype(BF16),
                )
    for r in range(nodes):
        place(r, pl.ds(2 * width, LANES), meta[r * cap : (r + 1) * cap].astype(BF16))

    pl.semaphore_wait(barrier, nodes - 1 + bits)

    arrived = {}
    buffers = {"rows": (rows, width), "ext": (ext, piece)}

    def pass_on(name, k, p, columns):
        buf, _ = buffers[name]
        for b in range(2, bits):
            if p < 1 << b:
                q = p + (1 << b)
                arrived.setdefault((name, k, q), []).append((columns, remote(
                    buf.at[k, p, :, columns], buf.at[k, q, :, columns], (n, l ^ masks[b])
                )))

    def own(name, k):
        buf, _ = buffers[name]
        for b in range(2):
            arrived[name, k, 1 << b] = [(None, remote(
                buf.at[k, 0], buf.at[k, 1 << b], (n, l ^ masks[b])
            ))]
        pass_on(name, k, 0, slice(None))

    def forward(name, k):
        buf, split = buffers[name]
        ends = buf.shape[-1]
        parts = (pl.ds(0, split), pl.ds(split, ends - split))
        for p, over in ((1, 1), (2, 0)):
            for _, copy in arrived[name, k, p]:
                copy.wait_recv()
            columns = parts[p - 1]
            arrived.setdefault((name, k, 3), []).append((columns, remote(
                buf.at[k, p, :, columns], buf.at[k, 3, :, columns], (n, l ^ masks[over])
            )))
            pass_on(name, k, p, slice(None))

    def corner(name, k):
        for p in range(3, local_count // 2):
            for columns, copy in list(arrived[name, k, p]):
                copy.wait_recv()
                pass_on(name, k, p, columns)

    def complete(name, k):
        for p in range(local_count // 2, local_count):
            for _, copy in arrived[name, k, p]:
                copy.wait_recv()

    entering = {}
    own("rows", 0)
    for k in range(1, nodes):
        r = order[k]
        entering["rows", k] = pltpu.make_async_remote_copy(
            src_ref=away.at[r - 1], dst_ref=rows.at[k, 0],
            send_sem=cross_send.at[k - 1], recv_sem=cross_recv.at[k - 1],
            device_id=(n ^ r, l), device_id_type=MESH,
        )
    for k in range(1, nodes):
        entering["rows", k].start()

    for r in range(nodes):
        start = pl.multiple_of((n ^ r) * piece, LANES)
        these = absent_b[r * rest : (r + 1) * rest]
        values = [
            (pl.ds(0, piece), dot(these, tok[:, pl.ds(start, piece)])),
            (pl.ds(piece, piece), dot(these, grad[:, pl.ds(start, piece)])),
            (pl.ds(2 * piece, LANES), meta_rest[r * rest : (r + 1) * rest]),
        ]
        for columns, value in values:
            if r == 0:
                ext[0, 0, :, columns] = value.astype(BF16)
            else:
                mine[r - 1, :, columns] = value.astype(BF16)

    def cross_ext():
        for k in range(1, nodes):
            r = order[k]
            entering["ext", k] = remote(mine.at[r - 1], ext.at[k, 0], (n ^ r, l))

    def enter(name, k):
        entering[name, k].wait_recv()
        own(name, k)

    expert = l // (local_count // E_NODE)
    deep = width // 7
    block = local_count * cap

    def chunk(k0, m, columns):
        return rows[k0 : k0 + m, :, :, columns].reshape(m * block, -1)

    def ffn(g):
        k0, m = spans[g]
        total = m * block
        pre[0:total, :] = jnp.zeros((total, 6 * units), F32)

        def step(c, carry):
            at = pl.multiple_of(c * deep, LANES)
            here = pl.ds(at, deep)
            pre[0:total, 0 : 4 * units] += dot(chunk(k0, m, here), w_in[here, :])
            left_g = chunk(k0, m, pl.ds(width + at, deep))
            pre[0:total, 4 * units :] += dot(left_g, w_out[here, :])
            return carry

        lax.fori_loop(0, 7, step, 0)
        table = chunk(k0, m, pl.ds(2 * width, LANES)).astype(F32)
        weight = jnp.where(expert == 0, table[:, 0:1], table[:, 1:2])
        is_shared = flag((iota((total, 1), 0) & (cap - 1)) < half)
        p, q, p_s, q_s, u, u_s = (pre[0:total, i * units : (i + 1) * units] for i in range(6))
        gg, gu, gh, product = ffn_backward(p, q, u, weight)
        sg, su, sh, _ = ffn_backward(p_s, q_s, u_s, is_shared)
        for i, value in enumerate((gg, gu, sg, su, gh)):
            grads[k0 * block : (k0 + m) * block, i * units : (i + 1) * units] = value
        score = jnp.sum(product, axis=1, keepdims=True)
        lanes = iota((total, LANES), 1)
        score = jnp.where(lanes == expert, score, 0.0)
        part[k0 : k0 + m, :, :, width:] = score.reshape(m, local_count, cap, LANES).astype(BF16)
        kept = m * seats
        shift, low = cap.bit_length() - 1, half.bit_length() - 1
        j, h = iota((kept, total), 0), iota((kept, total), 1)
        compact = flag(h == ((j >> low) << shift) + (j & (half - 1))).astype(BF16)
        for i, value in enumerate((sg, su, sh)):
            packs[0, k0 * seats : (k0 + m) * seats, i * units : (i + 1) * units] = dot(
                compact, value
            ).astype(BF16)

    turns = (dw_g, dw_u, dw_d, turned)

    def turn(i):
        loads[i].wait()
        eye = flag(iota((units, units), 0) == iota((units, units), 1)).astype(BF16)
        group = 4

        def step(c, carry):
            for sub in range(group):
                at = pl.ds(pl.multiple_of((c * group + sub) * units, LANES), units)
                turns[i][at, :] = contract_last(
                    eye, w_in[at, i * units : (i + 1) * units]
                ).astype(BF16)
            return carry

        lax.fori_loop(0, width // units // group, step, 0)

    def spread_dx(g, side):
        k0, m = spans[g]
        these = slice(k0 * block, (k0 + m) * block)
        group = 2
        count = width // 2 // units // group

        def step(c, carry):
            for sub in range(group):
                at = pl.ds(pl.multiple_of((c * group + sub) * units, LANES), units)
                total_dx = sum(
                    dot(grads[these, i * units : (i + 1) * units], turns[i][at, :])
                    for i in range(4)
                )
                part[k0 : k0 + m, :, :, at] = total_dx.reshape(m, local_count, cap, units).astype(
                    BF16
                )
            return carry

        lax.fori_loop(count * side, count * (side + 1), step, 0)

    def weight_grad(i, begin, end):
        base, first, outs = ((0, 0, (dw_g, dw_u)), (width, 4, (dw_d,)))[i]
        right = slice(first * units, (first + len(outs)) * units)
        size = deep // 2

        def step(c, carry):
            at = pl.multiple_of(c * size, LANES)
            left = chunk(0, nodes, pl.ds(base + at, size))
            both = contract_first(left, grads[:, right]).astype(BF16)
            for o, out in enumerate(outs):
                out[pl.ds(at, size), :] = both[:, o * units : (o + 1) * units]
            return carry

        lax.fori_loop(begin, end, step, 0)

    def arrange(name):
        source, out, size = {"rows": (rows, near, cap), "ext": (ext, far, rest)}[name]
        shift, low = cap.bit_length() - 1, half.bit_length() - 1
        slots, columns = nodes * cap, nodes * seats
        seat = local_count.bit_length() - 1 + low
        h, j = iota((slots, columns), 0), iota((slots, columns), 1)
        widen = flag(
            ((h >> shift) == (j >> seat)) & ((h & (cap - 1)) == (j & (half - 1)))
        ).astype(BF16)
        block_of = (iota((1, columns), 1) & (seats - 1)) >> low
        height = local_count * size
        owner = jnp.zeros((height, 1), I32)
        for p in range(1, local_count):
            owner = owner + jnp.where(iota((height, 1), 0) >= p * size, 1, 0)
        meta = source.shape[-1] - LANES
        for k in range(nodes):
            table = jnp.concatenate([
                packs[order.index(order[k] ^ r), order.index(r) * seats : (order.index(r) + 1) * seats, :]
                for r in range(nodes)
            ], axis=0)
            perm = source[k, :, :, meta:].reshape(height, LANES)[:, PERM : PERM + slots]
            full = jnp.where(owner == block_of, dot(perm, widen), 0.0).astype(BF16)
            out[k * height : (k + 1) * height, :] = dot(full, table).astype(BF16)

    waits, packed = [], []

    def send_packs(g):
        k0, m = spans[g]
        these = pl.ds(k0 * seats, m * seats)
        for k in range(1, nodes):
            packed.append(remote(packs.at[0, these], packs.at[k, these], (n ^ order[k], l)))

    full = part.shape[-1]
    cut = width // 2
    sides = (pl.ds(0, cut), pl.ds(cut, full - cut))
    flight = {}
    upper = bits - 2
    last = upper + 1

    def moves(side, stage):
        if stage < upper:
            b = bits - 1 - stage
            return [(1 << b, 1 << b)], masks[b], 1 << b
        first = stage == upper
        if side == 0:
            return ([(1, 1), (3, 1)], masks[0], 1) if first else ([(2, 1)], masks[1], 2)
        return ([(2, 2)], masks[1], 2) if first else ([(1, 1)], masks[0], 1)

    def reduce_start(g, side, stage):
        blocks, mask, _ = moves(side, stage)
        k0, m = spans[g]
        flight[g, side, stage] = [
            (k, p, size, remote(
                part.at[k, pl.ds(p, size), :, sides[side]],
                land.at[k, pl.ds(p, size), :, sides[side]], (n, l ^ mask),
            ))
            for k in range(k0, k0 + m) for p, size in blocks
        ]

    def reduce_settle(g, side, stage):
        _, _, gap = moves(side, stage)
        columns = sides[side]
        for k, p, size, copy in flight[g, side, stage]:
            copy.wait_recv()

            def add(i, carry, k=k, p=p):
                there = land[k, p + i, :, columns].astype(F32)
                here = part[k, p + i - gap, :, columns].astype(F32)
                part[k, p + i - gap, :, columns] = (here + there).astype(BF16)
                return carry

            lax.fori_loop(0, size, add, 0)

    def reduce_next(g, side, stage):
        reduce_settle(g, side, stage)
        if stage < last:
            reduce_start(g, side, stage + 1)

    def go_home(g, side):
        k0, m = spans[g]
        columns = sides[side]
        for k in range(k0, k0 + m):
            if k == 0:
                back[0, :, columns] = part[0, 0, :, columns]
            else:
                waits.append(remote(
                    part.at[k, 0, :, columns], back.at[order[k], :, columns], (n ^ order[k], l)
                ))

    half_way = spans[1][0]
    turn(0)
    turn(1)
    forward("rows", 0)
    turn(2)
    corner("rows", 0)
    enter("rows", 1)
    turn(3)
    forward("rows", 1)
    for k in range(2, half_way):
        enter("rows", k)
        forward("rows", k)
        corner("rows", k - 1)
    for k in range(half_way, nodes):
        enter("rows", k)
    corner("rows", half_way - 1)
    cross_ext()
    for load in loads[4:]:
        load.wait()
    for k in range(half_way):
        complete("rows", k)
    ffn(0)
    send_packs(0)
    for k in range(half_way, nodes - 1):
        forward("rows", k)
    spread_dx(0, 0)
    reduce_start(0, 0, 0)
    forward("rows", nodes - 1)
    for k in range(half_way, nodes - 1):
        corner("rows", k)
    spread_dx(0, 1)
    reduce_start(0, 1, 0)
    corner("rows", nodes - 1)
    for side in range(2):
        reduce_next(0, side, 0)
    own("ext", 0)
    for k in range(1, nodes):
        enter("ext", k)
    for k in range(half_way, nodes):
        complete("rows", k)
    ffn(1)
    send_packs(1)
    spread_dx(1, 0)
    reduce_start(1, 0, 0)
    for side in range(2):
        reduce_next(0, side, 1)
    spread_dx(1, 1)
    reduce_start(1, 1, 0)
    todo = [(i, b, min(b + 3 + i, 14)) for i in range(2) for b in range(0, 14, 3 + i)]

    def fill(count):
        for _ in range(min(count, len(todo))):
            weight_grad(*todo.pop(0))

    reduce_next(1, 0, 0)
    fill(1)
    reduce_next(1, 1, 0)
    for stage in range(2, last + 1):
        fill(3)
        for side in range(2):
            reduce_next(0, side, stage)
    for side in range(2):
        go_home(0, side)
    for stage in range(1, last):
        fill(2)
        for side in range(2):
            reduce_next(1, side, stage)
    for k in range(nodes):
        forward("ext", k)
    fill(2)
    reduce_next(1, 0, last)
    go_home(1, 0)
    fill(1)
    reduce_next(1, 1, last)
    go_home(1, 1)
    for k in range(nodes):
        corner("ext", k)
    fill(len(todo))
    for copy in packed:
        copy.wait_recv()
    arrange("rows")
    for k in range(nodes):
        complete("ext", k)
    arrange("ext")
    for copy in waits:
        copy.wait_recv()
    for k in range(1, nodes):
        entering["rows", k].wait_send()
    for copy in sends:
        copy.wait_send()


def room(scratch):
    held = sum(math.prod(dims) * jnp.dtype(kind).itemsize for dims, kind in scratch)
    return held + held // 32 + 2 * 2**20


def main_call(nodes, local_count, cap, tok, grad, ids, gates, weights):
    held, width = tok.shape
    units = weights[0].shape[1]
    rest, piece = held - cap, width // nodes
    most = max(m for _, m in spans_of(nodes)) * local_count * cap
    total = nodes * local_count * cap
    full, wide, narrow = width + LANES, 2 * width + LANES, 2 * piece + LANES
    vmem = pl.BlockSpec(memory_space=pltpu.VMEM)
    hbm = pl.BlockSpec(memory_space=pl.ANY)
    bits = local_count.bit_length() - 1
    gathers = 4 + sum(5 * 2 ** (b - 2) for b in range(2, bits))
    reduces = 2 * (bits - 2) + 5
    count = nodes * (2 * gathers + reduces) + (nodes - 1) * (3 + len(spans_of(nodes)))
    part = (nodes, local_count, cap, full)
    scratch = [
        ((nodes, total // 2, 3 * units), BF16),
        ((nodes - 1, cap, wide), BF16),
        ((nodes - 1, rest, narrow), BF16),
        ((width, 4 * units), BF16),
        ((width, 2 * units), BF16),
        ((width, units), BF16),
        (part, BF16),
        (part, BF16),
        ((most, 6 * units), F32),
        ((total, 5 * units), BF16),
    ]
    results = [
        (nodes, local_count, cap, wide),
        (nodes, local_count, rest, narrow),
        (total, 3 * units),
        (nodes * local_count * rest, 3 * units),
    ] + [(width, units)] * 3 + [(nodes, cap, full), (nodes * cap, held)]
    return pl.pallas_call(
        functools.partial(main_kernel, nodes, local_count, cap),
        out_shape=[pltpu.VMEM(dims, BF16) for dims in results],
        in_specs=[vmem] * 4 + [hbm] * 6,
        out_specs=[vmem] * 9,
        scratch_shapes=[pltpu.VMEM(*entry) for entry in scratch] + [
            pltpu.SemaphoreType.DMA((count,)),
            pltpu.SemaphoreType.DMA((count,)),
            pltpu.SemaphoreType.DMA((nodes - 1,)),
            pltpu.SemaphoreType.DMA((nodes - 1,)),
            pltpu.SemaphoreType.DMA((6,)),
        ],
        compiler_params=pltpu.CompilerParams(
            collective_id=0, has_side_effects=True, vmem_limit_bytes=room(scratch)
        ),
        name="exchange",
    )(tok, grad, ids, gates, *weights)


def finish_kernel(
    cap,
    rows, ext, near, far, dw_g, dw_u, dw_d, back, pick, ids,
    out_g, out_u, out_d, ds_g, ds_u, ds_d, dx, dgates,
    ds, sem,
):
    n = lax.axis_index("node")
    width, units = dw_g.shape
    piece = ds.shape[1]
    slots = pick.shape[0]
    copies = []

    def store(src, dst):
        copy = pltpu.make_async_copy(src, dst, sem.at[len(copies)])
        copy.start()
        copies.append(copy)

    for src, dst in ((dw_g, out_g), (dw_u, out_u), (dw_d, out_d)):
        store(src, dst)

    size = piece // 7
    for i, count in enumerate((2, 1)):
        cols = slice(2 * i * units, (2 * i + count) * units)

        def step(c, carry, i=i, cols=cols, count=count):
            at = pl.multiple_of(c * size, LANES)
            there = pl.multiple_of(i * width + n * piece + at, LANES)
            a = rows[:, :, :, pl.ds(there, size)].reshape(near.shape[0], size)
            b = ext[:, :, :, pl.ds(i * piece + at, size)].reshape(far.shape[0], size)
            value = contract_first(a, near[:, cols]) + contract_first(b, far[:, cols])
            for o in range(count):
                ds[2 * i + o, pl.ds(at, size), :] = value[
                    :, o * units : (o + 1) * units
                ].astype(BF16)
            return carry

        lax.fori_loop(0, 7, step, 0)
        for o in range(count):
            store(ds.at[2 * i + o], (ds_g, ds_u, ds_d)[2 * i + o])

    flat = back[...].reshape(slots, back.shape[-1])
    tile = width // 7
    for c in range(7):
        cols = slice(c * tile, (c + 1) * tile)
        dx[:, cols] = contract_first(pick[...], flat[:, cols]).astype(BF16)
    score = flat[:, width:].astype(F32)
    rel = (ids[...] >> 1) ^ n
    which = ids[...] & 1
    seen = pick[...].astype(F32)
    row_node = iota(seen.shape, 0) >> (cap.bit_length() - 1)
    total = jnp.zeros(dgates.shape, F32)
    for k in range(dgates.shape[0]):
        value = jnp.where(which[k : k + 1, :] == 0, score[:, 0:1], score[:, 1:2])
        value = jnp.where(row_node == rel[k : k + 1, :], seen * value, 0.0)
        value = jnp.sum(value, axis=0, keepdims=True)
        total = jnp.where(iota(dgates.shape, 0) == k, value, total)
    dgates[...] = total
    for copy in copies:
        copy.wait()


def finish_call(nodes, cap, values, ids):
    width, units = values[4].shape
    vmem = pl.BlockSpec(memory_space=pltpu.VMEM)
    hbm = pl.BlockSpec(memory_space=pl.ANY)
    shape = jax.ShapeDtypeStruct
    piece = width // nodes
    scratch = [((3, piece, units), BF16)]
    return pl.pallas_call(
        functools.partial(finish_kernel, cap),
        in_specs=[vmem] * 10,
        out_specs=[hbm] * 6 + [vmem] * 2,
        out_shape=[shape((width, units), BF16)] * 3 + [shape((piece, units), BF16)] * 3 + [
            shape((ids.shape[1], width), BF16), shape(ids.shape, F32),
        ],
        scratch_shapes=[pltpu.VMEM(*entry) for entry in scratch] + [
            pltpu.SemaphoreType.DMA((6,)),
        ],
        compiler_params=pltpu.CompilerParams(vmem_limit_bytes=room(scratch)),
        name="finish",
    )(*values, ids)


def local(tokens, grad_out, gates, expert_ids, w_gate, w_up, w_down, s_gate, s_up, s_down):
    held, width = tokens.shape
    nodes, locals_ = lax.axis_size("node"), lax.axis_size("local")
    cap = 2 * held // nodes
    weights = (w_gate[0], w_up[0], w_down[0], s_gate, s_up, s_down)
    ids = expert_ids.T
    values = main_call(nodes, locals_, cap, tokens, grad_out, ids, gates.T, weights)
    dw_g, dw_u, dw_d, ds_g, ds_u, ds_d, dx, dgates = finish_call(
        nodes, cap, values, ids
    )
    return (dx, dgates.T, dw_g[None], dw_u[None], dw_d[None], ds_g, ds_u, ds_d)


def solution(mesh):
    token = P(("node", "local"), None)
    routed = P("node", None, "local")
    shared = P(None, "local")
    shared_out = P("node", "local")
    return jax.shard_map(
        local,
        mesh=mesh,
        in_specs=(token,) * 4 + (routed,) * 3 + (shared,) * 3,
        out_specs=(token,) * 2 + (routed,) * 3 + (shared_out,) * 3,
        check_vma=False,
    )
```

time: 105 us -> 84.9 us (0.81)
  Pallas kernels: 100 us -> 84.1 us
  local copies, waits for them, and re-layouts: 4.06 us -> 0.01 us
    pallas_call x1, Pallas kernels: 15.2 us -> 6.11 us  [finish_call(): pl.pallas_call(functools.partial(finish_kernel, cap), in_specs=[vmem] * 1...]
    pallas_call x1, Pallas kernels: 84.9 us -> 77.9 us  [main_call(): pl.pallas_call(functools.partial(main_kernel, nodes, local_count, cap), o...]
    unnamed x3 -> x2, local copies, waits for them, and re-layouts: 4.06 us -> 0.01 us
where the time goes in v2:
time: 84.9 us; the launch traced here: 84.7 us
  Pallas kernels  84.1 us (99%)
    pallas_call x1, Pallas kernels, main_call(): pl.pallas_call(functools.partial(main_kernel, nodes, local_count, cap), o...  77.9 us
    pallas_call x1, Pallas kernels, finish_call(): pl.pallas_call(functools.partial(finish_kernel, cap), in_specs=[vmem] * 1...  6.11 us

profile of v2, /device:TPU:0, one launch (start us, length us, event | category | flops | bytes accessed | tf_op | source)
XLA Modules:
  0.0 84.7 jit_solution(12433028547114612472)
XLA Ops:
  0.6 0.0 copy-start
  0.6 77.9 %exchange.1 = (bf16[4,8,8,14464]{3,2,1,0:T(8,128)(2,1)S(1)}, bf16[4,8,8,3712]{3,2,1,0:T(8,128)(2,1)S(1)}, bf16[256,768]{1,0:T(8,128)(2,1)S(1)}, bf16[256,768]{1,...) custom-call(bf16[16,7168]{1,0:T(8,128)(2,1)} %tok.1, ...), custom_call_target="tpu_custom_call" | custom-call | tf_op jit(solution)/shard_map/exchange/pallas_call | solution.py:593
  78.6 0.0 copy-done
  78.6 6.1 %finish.1 = (bf16[7168,256]{1,0:T(8,128)(2,1)}, bf16[7168,256]{1,0:T(8,128)(2,1)}, bf16[7168,256]{1,0:T(8,128)(2,1)}, bf16[1792,256]{1,0:T(8,128)(2,1)}, bf16[17...) custom-call(bf16[4,8,8,14464]{3,2,1,0:T(8,128)(2,1)S(1)} %get-tuple-element.25.rows,, ...), custom_call_target="tpu_custom_call" | custom-call | tf_op jit(solution)/shard_map/finish/pallas_call | solution.py:680
Async XLA Ops:
  0.6 78.0 %copy-start = (s32[16,3]{0,1:T(4,128)S(1)}, s32[16,3]{0,1:T(4,128)}, u32[]{:S(2)}) copy-start(s32[16,3]{0,1:T(4,128)} %param.13) | copy-start | bytes 580

commit v3 on v2

--- a/solution.py
+++ b/solution.py
@@ -291,14 +291,14 @@
         pre[0:total, :] = jnp.zeros((total, 6 * units), F32)
 
         def step(c, carry):
-            at = pl.multiple_of(c * deep, LANES)
-            here = pl.ds(at, deep)
+            at = pl.multiple_of(c * (width // 2), LANES)
+            here = pl.ds(at, width // 2)
             pre[0:total, 0 : 4 * units] += dot(chunk(k0, m, here), w_in[here, :])
-            left_g = chunk(k0, m, pl.ds(width + at, deep))
+            left_g = chunk(k0, m, pl.ds(width + at, width // 2))
             pre[0:total, 4 * units :] += dot(left_g, w_out[here, :])
             return carry
 
-        lax.fori_loop(0, 7, step, 0)
+        lax.fori_loop(0, 2, step, 0)
         table = chunk(k0, m, pl.ds(2 * width, LANES)).astype(F32)
         weight = jnp.where(expert == 0, table[:, 0:1], table[:, 1:2])
         is_shared = flag((iota((total, 1), 0) & (cap - 1)) < half)
@@ -340,7 +340,7 @@
     def spread_dx(g, side):
         k0, m = spans[g]
         these = slice(k0 * block, (k0 + m) * block)
-        group = 2
+        group = 7
         count = width // 2 // units // group
 
         def step(c, carry):
@@ -360,7 +360,7 @@
     def weight_grad(i, begin, end):
         base, first, outs = ((0, 0, (dw_g, dw_u)), (width, 4, (dw_d,)))[i]
         right = slice(first * units, (first + len(outs)) * units)
-        size = deep // 2
+        size = deep
 
         def step(c, carry):
             at = pl.multiple_of(c * size, LANES)
@@ -420,24 +420,31 @@
             return ([(1, 1), (3, 1)], masks[0], 1) if first else ([(2, 1)], masks[1], 2)
         return ([(2, 2)], masks[1], 2) if first else ([(1, 1)], masks[0], 1)
 
-    def reduce_start(g, side, stage):
+    def members(g):
+        k0, m = spans[g]
+        return range(k0 + m - 1, k0 - 1, -1)
+
+    def launch(k, side, stage):
         blocks, mask, _ = moves(side, stage)
-        k0, m = spans[g]
-        flight[g, side, stage] = [
-            (k, p, size, remote(
+        flight[k, side, stage] = [
+            (p, size, remote(
                 part.at[k, pl.ds(p, size), :, sides[side]],
                 land.at[k, pl.ds(p, size), :, sides[side]], (n, l ^ mask),
             ))
-            for k in range(k0, k0 + m) for p, size in blocks
+            for p, size in blocks
         ]
 
-    def reduce_settle(g, side, stage):
+    def reduce_start(g, side):
+        for k in members(g):
+            launch(k, side, 0)
+
+    def settle(k, side, stage):
         _, _, gap = moves(side, stage)
         columns = sides[side]
-        for k, p, size, copy in flight[g, side, stage]:
+        for p, size, copy in flight[k, side, stage]:
             copy.wait_recv()
 
-            def add(i, carry, k=k, p=p):
+            def add(i, carry, p=p):
                 there = land[k, p + i, :, columns].astype(F32)
                 here = part[k, p + i - gap, :, columns].astype(F32)
                 part[k, p + i - gap, :, columns] = (here + there).astype(BF16)
@@ -445,38 +452,43 @@
 
             lax.fori_loop(0, size, add, 0)
 
-    def reduce_next(g, side, stage):
-        reduce_settle(g, side, stage)
+    def go_home(k, side):
+        columns = sides[side]
+        if k == 0:
+            back[0, :, columns] = part[0, 0, :, columns]
+        else:
+            waits.append(remote(
+                part.at[k, 0, :, columns], back.at[order[k], :, columns], (n ^ order[k], l)
+            ))
+
+    def reduce_next(k, side, stage):
+        settle(k, side, stage)
         if stage < last:
-            reduce_start(g, side, stage + 1)
-
-    def go_home(g, side):
-        k0, m = spans[g]
-        columns = sides[side]
-        for k in range(k0, k0 + m):
-            if k == 0:
-                back[0, :, columns] = part[0, 0, :, columns]
-            else:
-                waits.append(remote(
-                    part.at[k, 0, :, columns], back.at[order[k], :, columns], (n ^ order[k], l)
-                ))
+            launch(k, side, stage + 1)
+        else:
+            go_home(k, side)
+
+    def reduce_both(g, stage):
+        for k in members(g):
+            for side in range(2):
+                reduce_next(k, side, stage)
 
     half_way = spans[1][0]
     turn(0)
     turn(1)
     forward("rows", 0)
+    own("ext", 0)
     turn(2)
     corner("rows", 0)
-    enter("rows", 1)
+    for k in range(1, half_way):
+        enter("rows", k)
     turn(3)
-    forward("rows", 1)
-    for k in range(2, half_way):
-        enter("rows", k)
+    for k in range(1, half_way):
         forward("rows", k)
-        corner("rows", k - 1)
     for k in range(half_way, nodes):
         enter("rows", k)
-    corner("rows", half_way - 1)
+    for k in range(1, half_way):
+        corner("rows", k)
     cross_ext()
     for load in loads[4:]:
         load.wait()
@@ -487,55 +499,51 @@
     for k in range(half_way, nodes - 1):
         forward("rows", k)
     spread_dx(0, 0)
-    reduce_start(0, 0, 0)
+    reduce_start(0, 0)
     forward("rows", nodes - 1)
     for k in range(half_way, nodes - 1):
         corner("rows", k)
     spread_dx(0, 1)
-    reduce_start(0, 1, 0)
+    reduce_start(0, 1)
     corner("rows", nodes - 1)
-    for side in range(2):
-        reduce_next(0, side, 0)
-    own("ext", 0)
-    for k in range(1, nodes):
+    reduce_both(0, 0)
+    forward("ext", 0)
+    for k in range(1, half_way):
         enter("ext", k)
     for k in range(half_way, nodes):
         complete("rows", k)
     ffn(1)
     send_packs(1)
-    spread_dx(1, 0)
-    reduce_start(1, 0, 0)
     for side in range(2):
-        reduce_next(0, side, 1)
-    spread_dx(1, 1)
-    reduce_start(1, 1, 0)
-    todo = [(i, b, min(b + 3 + i, 14)) for i in range(2) for b in range(0, 14, 3 + i)]
+        spread_dx(1, side)
+        reduce_start(1, side)
+    todo = [(i, b, min(b + 1 + i, 7)) for i in range(2) for b in range(0, 7, 1 + i)]
 
     def fill(count):
         for _ in range(min(count, len(todo))):
             weight_grad(*todo.pop(0))
 
-    reduce_next(1, 0, 0)
+    reduce_both(0, 1)
+    for side in range(2):
+        for k in members(1):
+            reduce_next(k, side, 0)
+    for k in range(half_way, nodes):
+        enter("ext", k)
+    for stage in range(2, last + 1):
+        fill(4)
+        reduce_both(0, stage)
+    for stage in range(1, last):
+        for k in members(1):
+            for side in range(2):
+                reduce_next(k, side, stage)
+            fill(2)
+    for k in range(1, nodes):
+        forward("ext", k)
     fill(1)
-    reduce_next(1, 1, 0)
-    for stage in range(2, last + 1):
-        fill(3)
+    for k in members(1):
         for side in range(2):
-            reduce_next(0, side, stage)
-    for side in range(2):
-        go_home(0, side)
-    for stage in range(1, last):
-        fill(2)
-        for side in range(2):
-            reduce_next(1, side, stage)
-    for k in range(nodes):
-        forward("ext", k)
-    fill(2)
-    reduce_next(1, 0, last)
-    go_home(1, 0)
-    fill(1)
-    reduce_next(1, 1, last)
-    go_home(1, 1)
+            reduce_next(k, side, last)
+        fill(1)
     for k in range(nodes):
         corner("ext", k)
     fill(len(todo))
@@ -555,7 +563,7 @@
 
 def room(scratch):
     held = sum(math.prod(dims) * jnp.dtype(kind).itemsize for dims, kind in scratch)
-    return held + held // 32 + 2 * 2**20
+    return held + held // 32 + 3 * 2**20
 
 
 def main_call(nodes, local_count, cap, tok, grad, ids, gates, weights):

time: 84.9 us -> 79.7 us (0.939)
  Pallas kernels: 84.1 us -> 78.9 us
    pallas_call x1, Pallas kernels: 77.9 us -> 72.8 us  [main_call(): pl.pallas_call(functools.partial(main_kernel, nodes, local_count, cap), o...]
where the time goes in v3:
time: 79.7 us; the launch traced here: 79.6 us
  Pallas kernels  78.9 us (99%)
    pallas_call x1, Pallas kernels, main_call(): pl.pallas_call(functools.partial(main_kernel, nodes, local_count, cap), o...  72.8 us
    pallas_call x1, Pallas kernels, finish_call(): pl.pallas_call(functools.partial(finish_kernel, cap), in_specs=[vmem] * 1...  6.11 us

profile of v3, /device:TPU:0, one launch (start us, length us, event | category | flops | bytes accessed | tf_op | source)
XLA Modules:
  0.0 79.6 jit_solution(12474482883231122104)
XLA Ops:
  0.6 0.0 copy-start
  0.6 72.8 %exchange.1 = (bf16[4,8,8,14464]{3,2,1,0:T(8,128)(2,1)S(1)}, bf16[4,8,8,3712]{3,2,1,0:T(8,128)(2,1)S(1)}, bf16[256,768]{1,0:T(8,128)(2,1)S(1)}, bf16[256,768]{1,...) custom-call(bf16[16,7168]{1,0:T(8,128)(2,1)} %tok.1, ...), custom_call_target="tpu_custom_call" | custom-call | tf_op jit(solution)/shard_map/exchange/pallas_call | solution.py:601
  73.4 0.0 copy-done
  73.5 6.1 %finish.1 = (bf16[7168,256]{1,0:T(8,128)(2,1)}, bf16[7168,256]{1,0:T(8,128)(2,1)}, bf16[7168,256]{1,0:T(8,128)(2,1)}, bf16[1792,256]{1,0:T(8,128)(2,1)}, bf16[17...) custom-call(bf16[4,8,8,14464]{3,2,1,0:T(8,128)(2,1)S(1)} %get-tuple-element.25.rows,, ...), custom_call_target="tpu_custom_call" | custom-call | tf_op jit(solution)/shard_map/finish/pallas_call | solution.py:688
Async XLA Ops:
  0.6 72.8 %copy-start = (s32[16,3]{0,1:T(4,128)S(1)}, s32[16,3]{0,1:T(4,128)}, u32[]{:S(2)}) copy-start(s32[16,3]{0,1:T(4,128)} %param.13) | copy-start | bytes 580
